TPU v7x, 256 devices: a whole 4x4x8 slice. The times are simulated.
256 devices in a mesh: head: 64 (over x, z, y_lo), client: 4 (over y_hi, core).
Axes of the slice: x: 4, y: 4 (y_hi: 2, y_lo: 2; y = y_hi * 2 + y_lo), z: 8, core: 2. Of those that a mesh axis runs over, the one named last changes fastest.
Arguments:
- client_ids: int32 [256], replicated, may hold values from 0 to 1023, as said below
- client_table: bfloat16 [1024, 256], replicated, may hold values from -6 to 6
- in_weight: bfloat16 [256, 4096], P(None, 'client'), may hold values from -0.375 to 0.375
- in_bias: float32 [4096], P('client'), may hold values from -3 to 3
- head_weight: bfloat16 [4096, 131072], P('client', 'head'), may hold values from -0.09375 to 0.09375
- tokens: int32 [256, 256], P(('head', 'client')), may hold values from 0 to 255
- labels: int32 [256, 256], P(('head', 'client')), may hold values from 0 to 255
- byte_table: bfloat16 [256, 4096], P(None, 'client'), may hold values from -5.5 to 6.7
- out_table: bfloat16 [256, 4096], P(None, 'client'), may hold values from -5.625 to 5.625
Outputs:
- head_grad: bfloat16 [4096, 131072], P('client', 'head')
- in_grad: float32 [256, 4096], P(None, 'client')
- losses: float32 [256], P(('head', 'client'))
Inputs may be any that keep to these rules, and one draw needn't show every extreme that they name: `client_ids`: distinct population indices.
All inputs are finite; a program needn't handle non-finite values.
Results may differ from a plain program's by a relative error of at most 0.0085.
Values may be sent and summed in bfloat16 or wider, within the bound.
A program may use at most 64 MiB of HBM per device.

v0:
```python
import jax
import jax.numpy as jnp
from jax import lax
from jax.sharding import PartitionSpec as P

EPSILON = 1e-06
learn_rate = 0.1


def side_by_side(arrays, axis, dim, along):
    ends, at = ([], 0)
    for a in arrays[:-1]:
        at += a.shape[along]
        ends.append(at)
    both = jnp.concatenate(arrays, axis=along)
    return tuple(jnp.split(lax.all_gather(both, axis, axis=dim, tiled=True), ends, axis=along))


def cut_along(value, dim, length):
    before, after = (value.shape[:dim], value.shape[dim + 1 :])
    return jnp.moveaxis(value.reshape(*before, length, -1, *after), dim, 0)


def summed_on_arrival(value, axis, dim):
    pieces = cut_along(value, dim, lax.axis_size(axis))
    arrived = lax.all_to_all(pieces, axis, split_axis=0, concat_axis=0, tiled=True)
    return arrived.sum(axis=0)


def sent_to_all(value, axis):
    copies = jnp.broadcast_to(value, (lax.axis_size(axis), *value.shape))
    return lax.all_to_all(copies, axis, split_axis=0, concat_axis=0, tiled=True)


def laid_out(pieces, dim):
    lengths = list(pieces.shape[1:])
    lengths[dim] *= pieces.shape[0]
    return jnp.moveaxis(pieces, 0, dim).reshape(lengths)


def gather_directly(value, axis, dim):
    pieces = sent_to_all(value, axis)
    return laid_out(pieces, dim)


def sum_at_owner(value, axis, dim):
    pieces = cut_along(value, dim, lax.axis_size(axis))
    arrived = lax.all_to_all(pieces, axis, split_axis=0, concat_axis=0, tiled=True)
    return arrived.astype(jnp.float32).sum(axis=0)


def padded_to(lines, length):
    spare = -lines.shape[0] % length
    if not spare:
        return lines
    return jnp.concatenate([lines, jnp.zeros((spare, *lines.shape[1:]), lines.dtype)])


def nested_sum(value, axes):
    lines = value.reshape(-1, value.shape[-1])
    own = sum_at_owner(padded_to(lines, lax.axis_size(axes)), axes, 0)
    whole = gather_directly(own.astype(jnp.bfloat16), axes, 0)
    return whole[: len(lines)].reshape(value.shape).astype(jnp.float32)


def client_loss(factor_a, factor_b, inputs, label_row, out_table):
    depth = factor_a.shape[0]
    rank_size = factor_a.shape[1]
    normed_in = inputs * lax.rsqrt(jnp.mean(inputs * inputs, -1, keepdims=True) + EPSILON)
    low_rank = jnp.dot(normed_in, factor_a, precision=lax.Precision.HIGHEST)
    adapted = inputs + jnp.dot(low_rank, factor_b, precision=lax.Precision.HIGHEST) / jnp.sqrt(
        jnp.float32(depth * rank_size)
    )
    normed = (adapted * lax.rsqrt(jnp.mean(adapted * adapted, -1, keepdims=True) + EPSILON)).astype(
        jnp.bfloat16
    )
    logits = lax.dot_general(
        normed, out_table, (((1,), (1,)), ((), ())), preferred_element_type=jnp.float32
    )
    logits = logits * (4.0 / jnp.sqrt(jnp.float32(depth)))
    log_total = jax.nn.logsumexp(logits, -1)
    vocab_ids = lax.broadcasted_iota(jnp.int32, logits.shape, 1)
    picked = jnp.sum(jnp.where(vocab_ids == label_row[:, None], logits, 0.0), -1)
    return jnp.sum(log_total - picked)


def train_client(factor_row, token_row, label_row, byte_table, out_table):
    depth = byte_table.shape[1]
    split_at = factor_row.shape[0] // 2
    rank_size = split_at // depth
    start_a = factor_row[:split_at].reshape(depth, rank_size).astype(jnp.float32)
    start_b = factor_row[split_at:].reshape(rank_size, depth).astype(jnp.float32)
    onehot = (
        token_row[:, None]
        == lax.broadcasted_iota(jnp.int32, (token_row.shape[0], byte_table.shape[0]), 1)
    ).astype(jnp.bfloat16)
    inputs = jnp.dot(onehot, byte_table, preferred_element_type=jnp.float32)
    loss_grad = jax.value_and_grad(client_loss, argnums=(0, 1))
    first_loss, (grad_a, grad_b) = loss_grad(start_a, start_b, inputs, label_row, out_table)
    middle_a = start_a - learn_rate * grad_a
    middle_b = start_b - learn_rate * grad_b
    second_loss, (grad_a, grad_b) = loss_grad(middle_a, middle_b, inputs, label_row, out_table)
    final_a = middle_a - learn_rate * grad_a
    final_b = middle_b - learn_rate * grad_b
    deltas = jnp.concatenate(
        [(final_a - start_a).reshape(-1), (final_b - start_b).reshape(-1)]
    ).astype(jnp.bfloat16)
    return (deltas, first_loss / token_row.shape[0])


def local(
    client_ids, client_table, in_weight, in_bias, head_weight, tokens, labels, byte_table, out_table
):
    head_count = lax.axis_size("head")
    group_count = lax.axis_size("client")
    per_device = tokens.shape[0]
    byte_full, out_full = side_by_side((byte_table, out_table), "client", 1, 0)
    ordered = client_ids.reshape(head_count, group_count, per_device).transpose(1, 0, 2).reshape(-1)
    chosen = client_table[ordered]
    preact = jnp.dot(chosen, in_weight, preferred_element_type=jnp.float32) + in_bias
    hidden = jnp.maximum(preact, 0.0).astype(jnp.bfloat16)
    hidden_rows = hidden
    summed = summed_on_arrival(
        jnp.dot(hidden_rows, head_weight, preferred_element_type=jnp.float32), "client", 0
    )
    owned = lax.all_to_all(
        summed.astype(jnp.bfloat16), "head", split_axis=0, concat_axis=1, tiled=True
    )

    def run_client(record):
        return train_client(record[0], record[1], record[2], byte_full, out_full)

    deltas, losses = lax.map(run_client, (owned, tokens, labels))
    returned = lax.all_to_all(deltas, "head", split_axis=1, concat_axis=0, tiled=True)
    received = gather_directly(returned, "client", 0)
    hidden_rows = hidden
    grad_sum = lax.dot_general(
        hidden_rows, received, (((0,), (0,)), ((), ())), preferred_element_type=jnp.float32
    )
    partial_value = lax.dot_general(
        received, head_weight, (((1,), (1,)), ((), ())), preferred_element_type=jnp.float32
    )
    hidden_back = partial_value
    grad_sum, hidden_back = (grad_sum, hidden_back)
    hidden_back = nested_sum(hidden_back.astype(jnp.bfloat16), "head")
    masked = jnp.where(preact > 0, hidden_back, 0.0)
    in_grad = lax.dot_general(
        chosen.astype(jnp.float32),
        masked,
        (((0,), (0,)), ((), ())),
        precision=lax.Precision.HIGHEST,
    )
    return (grad_sum.astype(jnp.bfloat16), in_grad, losses)


def solution(mesh):
    placed = (
        P(),
        P(),
        P(None, "client"),
        P("client"),
        P("client", "head"),
        P(("head", "client"), None),
        P(("head", "client"), None),
        P(None, "client"),
        P(None, "client"),
    )
    return jax.shard_map(
        local,
        mesh=mesh,
        in_specs=placed,
        out_specs=(P("client", "head"), P(None, "client"), P(("head", "client"))),
        check_vma=False,
    )
```

profile of v0, /device:TPU:2, one launch (start us, length us, event | category | flops | bytes accessed | tf_op | source)
XLA Modules:
  0.0 234.9 jit_solution(666973814502841512)
XLA Ops:
  7.2 0.0 copy-start
  7.2 0.0 all-gather.2.cloned.1.call-start
  7.2 2.3 pad_maximum_fusion
  9.5 0.0 all-gather.2.cloned.1.call-update
  9.5 0.8 reshape.186
  10.3 0.1 copy.19
  10.4 0.1 reshape.187
  10.5 2.1 gather_fusion
  12.6 0.0 copy-done
  12.6 0.0 copy-done.5
  12.6 0.3 convolution_add_fusion
  12.9 3.4 %fusion.52 = f32[256,2048]{1,0:T(8,128)S(1)} fusion(bf16[1024,2048]{1,0:T(8,128)(2,1)} %param.13, f32[256,1024]{1,0:T(8,128)S(1)} %convolution_add_fusion), kind=kOutput, calls=%fused_computation.83 | convolution fusion | flops 1074266112 | bytes 7340032 | tf_op jit(solution)/shard_map/dot_general | solution.py:124
  16.4 49.5 %all_to_all.43 = f32[4,64,2048]{2,1,0:T(8,128)} all-to-all(f32[4,64,2048]{2,1,0:T(8,128)S(1)} %bitcast.38), channel_id=1, replica_groups=mesh['head'=64,'client'=4] {'client'}, dimensions={0} | all-to-all | bytes 4194304 | tf_op jit(solution)/shard_map/all_to_all | solution.py:26
  65.9 1.8 reduce_sum.125
  67.7 0.5 broadcast.217
  68.2 0.8 reduce.5
  69.0 0.2 reshape.204
  69.2 24.3 %all_to_all.44 = bf16[64,2,1024]{2,1,0:T(2,128)(2,1)S(1)} all-to-all(bf16[64,2,1024]{2,1,0:T(2,128)(2,1)S(1)} %reshape.204), channel_id=1, replica_groups=mesh['head'=64,'client'=4] {'head'}, dimensions={0} | all-to-all | bytes 524288 | tf_op jit(solution)/shard_map/all_to_all | solution.py:126
  93.4 0.7 reshape.205
  94.1 1.1 slice_reduce_fusion
  95.3 0.8 reshape.189
  96.1 0.3 copy.21
  96.4 0.0 all-gather.2.cloned.1.call-done
  96.4 2.4 %multiply_reduce_fusion.2 = (f32[256]{0:T(256)S(1)}, f32[256,4096]{1,0:T(8,128)S(1)}) fusion(bf16[512,4096]{1,0:T(8,128)(2,1)} %all-gather.2.cloned.1.call-done, s32[256]{0:T(256)S(1)} %bitcast.46), kind=kOutput, calls=%fused_computation.33 | convolution fusion | flops 539033344 | bytes 6293504 | tf_op jit(solution)/shard_map/while/body/eval_jaxpr/dot_general | solution.py:97
  98.9 2.3 fusion.18
  101.2 2.4 %multiply_reduce_fusion.1 = (f32[256]{0:T(256)S(1)}, f32[256,4096]{1,0:T(8,128)S(1)}) fusion(f32[256,4096]{1,0:T(8,128)S(1)} %get-tuple-element.34, f32[256,16]{0,1:T(8,128)S(1)} %fusion.18, bf16[16,4096]{1,0:T(8,128)(2,1)S(1)} %reshape.190), kind=kOutput, calls=%fused_computation.32 | convolution fusion | flops 205520640 | bytes 8537088 | tf_op jit(solution)/shard_map/while/body/eval_jaxpr/jvp()/dot_general | solution.py:71
  103.6 0.0 copy-start.4
  103.7 0.8 fusion.83
  104.5 0.1 select_reduce_fusion
  104.6 0.6 subtract_reduce_fusion
  105.2 0.9 fusion.10
  106.1 2.8 %fusion.81 = f32[256,16]{0,1:T(8,128)S(1)} fusion(bf16[16,4096]{1,0:T(8,128)(2,1)S(1)} %reshape.190, bf16[256,4096]{1,0:T(8,128)(2,1)S(1)} %get-tuple-element.40, f32[256,4096]{1,0:T(8,128)S(1)} %get-tuple-element.36, f32[256]{0:T(256)S(1)} %multiply_multiply_fusion.1, f32[256]{0:T(256)S(1)} %fusion.66), kind=kOutput, calls=%fused_computation.121 | convolution fusion | flops 207618048 | bytes 6440960 | tf_op jit(solution)/shard_map/while/body/eval_jaxpr/transpose(jvp())/dot_general | solution.py:71
  109.0 3.1 %fusion.6 = f32[16,4096]{1,0:T(8,128)S(1)} fusion(f32[256,16]{0,1:T(8,128)S(1)} %fusion.18, bf16[16,4096]{1,0:T(8,128)(2,1)S(1)} %reshape.190, bf16[256,4096]{1,0:T(8,128)(2,1)S(1)} %get-tuple-element.40, f32[256,4096]{1,0:T(8,128)S(1)} %get-tuple-element.36, f32[256]{0:T(256)S(1)} %multiply_multiply_fusion.1, f32[256]{0:T(256)S(1)} %fusion.66), kind=kOutput, calls=%fused_computation.20 | convolution fusion | flops 207814656 | bytes 6703104 | tf_op jit(solution)/shard_map/while/body/eval_jaxpr/transpose(jvp())/dot_general | solution.py:71
  112.1 2.5 %fusion.7 = f32[4096,16]{0,1:T(8,128)S(1)} fusion(f32[256,16]{0,1:T(8,128)S(1)} %fusion.81, f32[256,4096]{1,0:T(8,128)S(1)} %get-tuple-element.34, f32[256]{0:T(256)S(1)} %add_rsqrt_fusion, bf16[4096,16]{0,1:T(8,128)(2,1)S(1)} %copy.21), kind=kOutput, calls=%fused_computation.22 | convolution fusion | flops 202571776 | bytes 4604928 | tf_op jit(solution)/shard_map/while/body/eval_jaxpr/transpose(jvp())/dot_general | solution.py:70
  114.6 3.4 %fusion.15 = f32[256,16]{0,1:T(8,128)S(1)} fusion(f32[4096,16]{0,1:T(8,128)S(1)} %fusion.7, f32[256,4096]{1,0:T(8,128)S(1)} %get-tuple-element.34, f32[256]{0:T(256)S(1)} %add_rsqrt_fusion), kind=kOutput, calls=%fused_computation.36 | convolution fusion | flops 202375168 | bytes 4473856 | tf_op jit(solution)/shard_map/while/body/eval_jaxpr/jvp()/dot_general | solution.py:70
  118.0 4.1 %multiply_reduce_fusion = (f32[256]{0:T(256)S(1)}, f32[256,4096]{1,0:T(8,128)S(1)}) fusion(f32[256,4096]{1,0:T(8,128)S(1)} %get-tuple-element.34, f32[256,16]{0,1:T(8,128)S(1)} %fusion.15, f32[16,4096]{1,0:T(8,128)S(1)} %fusion.6), kind=kOutput, calls=%fused_computation.30 | convolution fusion | flops 205520640 | bytes 8668160 | tf_op jit(solution)/shard_map/while/body/eval_jaxpr/jvp()/dot_general | solution.py:71
  122.2 0.9 fusion.84
  123.0 0.1 fusion.51
  123.1 1.1 fusion.11
  124.3 3.0 %fusion.9 = bf16[16,4096]{1,0:T(8,128)(2,1)S(1)} fusion(f32[16,4096]{1,0:T(8,128)S(1)} %fusion.6, f32[256,16]{0,1:T(8,128)S(1)} %fusion.15, bf16[16,4096]{1,0:T(8,128)(2,1)S(1)} %reshape.190, bf16[256,4096]{1,0:T(8,128)(2,1)S(1)} %get-tuple-element.46, f32[256,4096]{1,0:T(8,128)S(1)} %get-tuple-element.42, f32[256]{0:T(256)S(1)} %multiply_multiply_fusion, ...), kind=kOutput, calls=%fused_computation.24 | convolution fusion | flops 207945728 | bytes 6834176 | tf_op jit(solution)/shard_map/while/body/eval_jaxpr/transpose(jvp())/dot_general | solution.py:71
  127.2 4.0 %fusion.78 = f32[256,16]{0,1:T(8,128)S(1)} fusion(f32[16,4096]{1,0:T(8,128)S(1)} %fusion.6, bf16[256,4096]{1,0:T(8,128)(2,1)S(1)} %get-tuple-element.46, f32[256,4096]{1,0:T(8,128)S(1)} %get-tuple-element.42, f32[256]{0:T(256)S(1)} %multiply_multiply_fusion, f32[256]{0:T(256)S(1)} %fusion.67), kind=kOutput, calls=%fused_computation.120 | convolution fusion | flops 207618048 | bytes 6572032 | tf_op jit(solution)/shard_map/while/body/eval_jaxpr/transpose(jvp())/dot_general | solution.py:71
  131.2 2.5 %fusion.8 = bf16[4096,16]{0,1:T(8,128)(2,1)S(1)} fusion(f32[4096,16]{0,1:T(8,128)S(1)} %fusion.7, f32[256,16]{0,1:T(8,128)S(1)} %fusion.78, f32[256,4096]{1,0:T(8,128)S(1)} %get-tuple-element.34, f32[256]{0:T(256)S(1)} %add_rsqrt_fusion, bf16[4096,16]{0,1:T(8,128)(2,1)S(1)} %copy.21), kind=kOutput, calls=%fused_computation.23 | convolution fusion | flops 202702848 | bytes 4736000 | tf_op jit(solution)/shard_map/while/body/eval_jaxpr/transpose(jvp())/dot_general | solution.py:70
  133.7 0.1 concatenate.22
  133.8 0.5 copy.22
  134.3 1.8 concatenate.21
  136.1 0.4 copy.28
  136.5 2.4 %reduce.6 = bf16[64,2048]{1,0:T(8,128)(2,1)S(1)} reduce(bf16[64,1,2048]{2,1,0:T(2,128)(2,1)S(1)} %bitcast.42, bf16[]{:T(256)} %broadcast.217), dimensions={1}, to_apply=%bitcast.37.reduce_sub_computation | reduce | bytes 524290
  138.9 0.2 reshape.206
  139.1 17.0 %all_to_all.45 = bf16[64,2,1024]{2,1,0:T(2,128)(2,1)S(1)} all-to-all(bf16[64,2,1024]{2,1,0:T(2,128)(2,1)S(1)} %reshape.206), channel_id=1, replica_groups=mesh['head'=64,'client'=4] {'head'}, dimensions={0} | all-to-all | bytes 524288 | tf_op jit(solution)/shard_map/all_to_all | solution.py:134
  156.1 0.2 reshape.207
  156.3 0.0 copy-start.2
  156.3 0.2 copy.27
  156.5 0.1 broadcast_in_dim.64
  156.6 18.6 %all_to_all.46 = bf16[4,64,2048]{2,1,0:T(8,128)(2,1)S(1)} all-to-all(bf16[4,64,2048]{2,1,0:T(8,128)(2,1)S(1)} %broadcast_in_dim.64), channel_id=1, replica_groups=mesh['head'=64,'client'=4] {'client'}, dimensions={0} | all-to-all | bytes 2097152 | tf_op jit(solution)/shard_map/all_to_all | solution.py:32
  175.2 1.3 convolution_convert_fusion.3
  176.5 1.0 reshape.192
  177.5 22.9 %all_to_all.47 = bf16[64,4,1024]{2,1,0:T(4,128)(2,1)S(1)} all-to-all(bf16[64,4,1024]{2,1,0:T(4,128)(2,1)} %reshape.192), channel_id=1, replica_groups=mesh['head'=64,'client'=4] {'head'}, dimensions={0} | all-to-all | bytes 1048576 | tf_op jit(solution)/shard_map/all_to_all | solution.py:48
  200.4 0.2 reduce_sum.133
  200.6 0.9 broadcast_in_dim.65
  201.6 6.8 %all-to-all-start.5 = ((bf16[64,4,1024]{2,1,0:T(4,128)(2,1)}), bf16[64,4,1024]{2,1,0:T(4,128)(2,1)S(1)}, u32[]{:S(2)}, u32[]{:S(2)}) async-start(bf16[64,4,1024]{2,1,0:T(4,128)(2,1)} %broadcast_in_dim.65), calls=%async_computation.5 | async-start | bytes 1048576 | tf_op jit(solution)/shard_map/all_to_all | solution.py:32
  209.1 3.3 %convolution_convert_fusion.2 = bf16[1024,2048]{1,0:T(8,128)(2,1)} fusion(bf16[256,2048]{1,0:T(8,128)(2,1)S(1)} %bitcast.40, f32[256,1024]{1,0:T(8,128)S(1)} %convolution_add_fusion), kind=kOutput, calls=%fused_computation.34 | convolution fusion | flops 1076363264 | bytes 6291456 | tf_op jit(solution)/shard_map/dot_general | solution.py:137
  212.4 12.3 %all-to-all-done.5 = bf16[64,4,1024]{2,1,0:T(4,128)(2,1)S(1)} async-done(((bf16[64,4,1024]{2,1,0:T(4,128)(2,1)}), bf16[64,4,1024]{2,1,0:T(4,128)(2,1)S(1)}, u32[]{:S(2)}, u32[]{:S(2)}) %all-to-all-start.5) | async-done | bytes 524320 | tf_op jit(solution)/shard_map/all_to_all | solution.py:32
  224.7 0.1 reshape.193
  224.7 1.7 fusion.40
  (19 shorter events, 0.2 us)
Async XLA Ops:
  7.2 5.4 %copy-start = (bf16[256,1024]{1,0:T(8,128)(2,1)S(1)}, bf16[256,1024]{1,0:T(8,128)(2,1)}, u32[]{:S(2)}) copy-start(bf16[256,1024]{1,0:T(8,128)(2,1)} %param.11) | copy-start | bytes 1572868
  7.2 5.4 %copy-start.5 = (f32[1024]{0:T(1024)S(1)}, f32[1024]{0:T(1024)}, u32[]{:S(2)}) copy-start(f32[1024]{0:T(1024)} %param.12) | copy-start | bytes 12292
  7.2 89.2 %all-gather.2.cloned.1.call-start = ((), (), s32[]{:S(2)}) async-start(), calls=%async_computation.6 | async-start | bytes 5242880 | tf_op jit(solution)/shard_map/all_gather | solution.py:16
  65.9 30.6 %copy-start.3 = (s32[1,256]{1,0:T(1,128)S(1)}, s32[1,256]{1,0:T(1,128)}, u32[]{:S(2)}) copy-start(s32[1,256]{1,0:T(1,128)} %param.14) | copy-start | bytes 3076
  101.2 2.5 %copy-start.1 = (bf16[512,4096]{1,0:T(8,128)(2,1)S(1)}, bf16[512,4096]{1,0:T(8,128)(2,1)}, u32[]{:S(2)}) copy-start(bf16[512,4096]{1,0:T(8,128)(2,1)} %all-gather.2.cloned.1.call-done) | copy-start | bytes 12582916
  103.6 0.9 copy-start.4
  156.3 18.9 %copy-start.2 = (bf16[1024,2048]{1,0:T(8,128)(2,1)S(1)}, bf16[1024,2048]{1,0:T(8,128)(2,1)}, u32[]{:S(2)}) copy-start(bf16[1024,2048]{1,0:T(8,128)(2,1)} %param.13) | copy-start | bytes 12582916
  201.6 23.1 %all-to-all-start.5 = ((bf16[64,4,1024]{2,1,0:T(4,128)(2,1)}), bf16[64,4,1024]{2,1,0:T(4,128)(2,1)S(1)}, u32[]{:S(2)}, u32[]{:S(2)}) async-start(bf16[64,4,1024]{2,1,0:T(4,128)(2,1)} %broadcast_in_dim.65), calls=%async_computation.5 | async-start | bytes 1048576 | tf_op jit(solution)/shard_map/all_to_all | solution.py:32
Sparse Core Ops, SparseCore 0:
  10.4 61.4 all-gather.1
where the time goes:
time: 239 us; the launch traced here: 235 us
  blocking collectives  132 us (55%)
  matrix products  46.4 us (19%)
  between operations  16.5 us (7%)
  waiting for transfers between devices  12.3 us (5%)
  local copies, waits for them, and re-layouts  12.1 us (5%)
  other arithmetic  8.39 us (4%)
  starting transfers between devices  6.88 us (3%)
    all_to_all x1, blocking collectives, summed_on_arrival(): lax.all_to_all(pieces, axis, split_axis=0, concat_axis=0, tiled=True)  49.5 us
    all_to_all x1, blocking collectives, local(): lax.all_to_all(summed.astype(jnp.bfloat16), 'head', split_axis=0, concat_...  24.3 us
    all_to_all x1, blocking collectives, sum_at_owner(): lax.all_to_all(pieces, axis, split_axis=0, concat_axis=0, tiled=True)  22.9 us
    dot_general x6, matrix products, client_loss(): jnp.dot(low_rank, factor_b, precision=lax.Precision.HIGHEST)  19.5 us
    all_to_all x1, blocking collectives, sent_to_all(): return lax.all_to_all(copies, axis, split_axis=0, concat_axis=0, tiled=True)  18.6 us
    all_to_all x1, blocking collectives, local(): lax.all_to_all(deltas, 'head', split_axis=1, concat_axis=0, tiled=True)  17 us
    all_to_all x1, waiting for transfers between devices, sent_to_all(): return lax.all_to_all(copies, axis, split_axis=0, concat_axis=0, tiled=True)  12.3 us
    dot_general x4, matrix products, client_loss(): low_rank = jnp.dot(normed_in, factor_a, precision=lax.Precision.HIGHEST)  10.8 us
  transfers between devices with their start and end apart: 2, of which 1 were waited for; matrix products, arithmetic and copies ran while one was open for 7% of the time, Pallas kernels for 0%

commit v1 on v0

v1 whole, which is shorter than its diff:
```python
import jax
import jax.numpy as jnp
from jax import lax
from jax.experimental import pallas as pl
from jax.experimental.pallas import tpu as pltpu
from jax.sharding import PartitionSpec as P

EPS = 1e-6
ETA = 0.1
F32 = jnp.float32
BF = jnp.bfloat16
MESH = pl.DeviceIdType.MESH
CH = 4
CW = 2048 // CH


def mm(a, b, ca, cb):
    return lax.dot_general(
        a.astype(BF), b.astype(BF), (((ca,), (cb,)), ((), ())), preferred_element_type=F32
    )


def iota(shape, dim):
    return lax.broadcasted_iota(jnp.int32, shape, dim)


def gradients(pt, qt, rt, s_mat, obt, bb, scale, ct, cnt):
    tt = pt * (scale * (1 / 256))
    st = mm(s_mat, tt, 1, 0)
    msq = (bb + jnp.sum(tt * (2 * rt + st), 0, keepdims=True)) * (1 / 4096)
    q = lax.rsqrt(msq + EPS)
    mt = obt + mm(qt, tt, 0, 0)
    lg = mt * (q * (1 / 16))
    top = jnp.max(lg, 0, keepdims=True)
    ex = jnp.exp(lg - top)
    total = jnp.sum(ex, 0, keepdims=True)
    gt = (ex * (cnt / total) - ct) * (1 / 16)
    along = jnp.sum(gt * mt, 0, keepdims=True)
    e = q * q * q * along * (1 / 4096)
    ht = gt * q
    dt = mm(qt, ht, 1, 0) - e * (rt + st)
    ut = dt * (scale * (1 / 256))
    xt = mm(tt, ht, 1, 1)
    yt = tt * e
    z = mm(yt, tt, 1, 1)
    loss = jnp.sum(cnt * (top + jnp.log(total)) - jnp.sum(ct * lg, 0, keepdims=True))
    return ut, xt, yt, z, loss


def two_steps(pt, qt, rt, s_mat, obt, oo, bbm, bb, scale, ct, cnt):
    u1, x1, y1, z1, loss = gradients(pt, qt, rt, s_mat, obt, bb, scale, ct, cnt)
    vo = -ETA * mm(x1, oo, 1, 0) + ETA * mm(y1, obt, 1, 1)
    vb = -ETA * mm(x1, obt, 1, 0) + ETA * mm(y1, bbm, 1, 0)
    z1 = ETA * z1
    p2 = pt - ETA * mm(u1, bbm, 1, 0)
    q2 = qt + mm(z1, qt, 1, 0) + vo
    r2 = rt + mm(z1, rt, 1, 0) + vb
    h = -ETA * mm(qt, x1, 1, 1) + ETA * mm(rt, y1, 1, 1)
    ht = -ETA * mm(x1, qt, 1, 1) + ETA * mm(y1, rt, 1, 1)
    vv = -ETA * mm(x1, vo, 1, 1) + ETA * mm(y1, vb, 1, 1)
    zs = mm(z1, s_mat, 1, 0)
    s2 = s_mat + zs + mm(s_mat, z1, 1, 1) + mm(zs, z1, 1, 1)
    s2 = s2 + h + mm(z1, h, 1, 0) + ht + mm(ht, z1, 1, 1) + vv
    u2, x2, y2, z2, _ = gradients(p2, q2, r2, s2, obt, bb, scale, ct, cnt)
    z2 = ETA * z2
    u = -ETA * (u1 + u2)
    x = -ETA * (x1 + mm(z2, x1, 1, 0) + x2)
    y = ETA * (y1 + mm(z2, y1, 1, 0) + y2)
    z = z1 + z2 + mm(z2, z1, 1, 0)
    return u, x, y, z, loss


def kernel(
    ids, table, inw, bias, w_hbm, tok, lab, byte, outt,
    ing_o, dn, hid, loss_o,
    w, fs, fr, sb, r2, ft, f, rx, la, lb, xf, bp, gp, gq, gn, ms, er, cm, cr, ta, tx, g_in, d_in,
    hb, a1, a1s, a2, ag, hidt, chosen_s,
    sw, r1s, r1r, r2s, r2r, gss, gsr, r3s, r3r, e1s, e1r, e2s, e2r, r4s, r4r, r5s, r5r, r6s, r6r,
    p1s, p1r, p2s, p2r, p3s, p3r, p4s, p4r,
):
    head = lax.axis_index("head")
    grp = lax.axis_index("client")
    x, z, lo = head // 16, (head // 2) % 8, head % 2
    hi, k = grp // 2, grp % 2
    p = (hi + lo) % 2

    def dev(x_, z_, lo_, hi_, k_):
        return (x_ * 16 + z_ * 2 + lo_, hi_ * 2 + k_)

    def remote(src, dst, ss, rs, to):
        return pltpu.make_async_remote_copy(
            src_ref=src, dst_ref=dst, send_sem=ss, recv_sem=rs, device_id=to, device_id_type=MESH
        )

    partner = dev(x, z, lo, hi, 1 - k)
    n1 = dev(x, z, 1 - lo, hi, k)
    n2 = dev(x, z, 1 - lo, 1 - hi, k)

    wc = []
    for i in range(CH):
        c = pltpu.make_async_copy(
            w_hbm.at[:, pl.ds(i * CW, CW)], w.at[:, pl.ds(i * CW, CW)], sw.at[i]
        )
        c.start()
        wc.append(c)

    bar = pltpu.get_barrier_semaphore()

    def greet(i, _):
        x_, z_ = i // 32, (i // 4) % 8
        hi_, k_ = (i // 2) % 2, i % 2
        lo_ = (p + hi_) % 2
        same = (x_ == x) & (z_ == z) & (hi_ == hi) & (k_ == k)

        @pl.when(jnp.logical_not(same))
        def _():
            pl.semaphore_signal(bar, inc=1, device_id=dev(x_, z_, lo_, hi_, k_), device_id_type=MESH)

        return 0

    lax.fori_loop(0, 128, greet, 0)
    for dx in range(4):
        pl.semaphore_signal(
            bar, inc=1, device_id=dev((x + dx) % 4, z, 1 - lo, hi, k), device_id_type=MESH
        )

    m = iota((256, 256), 1)
    mhi, mxz, mp, mk = m % 2, (m // 2) % 32, (m // 64) % 2, m // 128
    owner = (mxz * 2 + (mp + mhi) % 2) * 4 + mhi * 2 + mk
    order = (iota((256, 256), 0) == owner).astype(BF)
    picks = (iota((1024, 256), 0) == ids[...]).astype(F32).astype(BF)
    picks = mm(picks, order, 1, 0)
    chosen = mm(picks, table[...], 0, 0).astype(BF)
    chosen_s[...] = chosen
    pre = mm(chosen, inw[...], 1, 0) + bias[...]
    hidden = jnp.maximum(pre, 0.0)
    hid[...] = hidden.astype(BF)

    pl.semaphore_wait(bar, 131)

    c1 = []
    for i in range(CH):
        cols = pl.ds(i * CW, CW)
        wc[i].wait()
        fs[:, cols] = jnp.dot(hid[...], w[:, cols], preferred_element_type=F32)
        c = remote(
            fs.at[pl.ds((1 - k) * 128, 128), cols], fr.at[:, cols], r1s.at[i], r1r.at[i], partner
        )
        c.start()
        c1.append(c)
    c2 = []
    for i in range(CH):
        cols = pl.ds(i * CW, CW)
        c1[i].wait_recv()
        sb[:, cols] = (fs[pl.ds(pl.multiple_of(k * 128, 128), 128), cols] + fr[:, cols]).astype(BF)
        a = remote(
            sb.at[pl.ds((1 - p) * 64, 64), cols], r2.at[0, :, cols], r2s.at[0, i], r2r.at[0, i], n1
        )
        b = remote(
            sb.at[pl.ds(p * 64, 64), cols], r2.at[1, :, cols], r2s.at[1, i], r2r.at[1, i], n2
        )
        a.start()
        b.start()
        c2.append((a, b))

    gp[0:256, :] = mm(outt[...], byte[...], 1, 1)
    gp[256:512, :] = mm(outt[...], outt[...], 1, 1)
    gp[512:768, :] = mm(byte[...], byte[...], 1, 1)
    cg = remote(gp, gq, gss.at[0], gsr.at[0], partner)
    cg.start()
    for d8 in range(8):
        perm = (iota((1024, 128), 0) == 8 * iota((1024, 128), 1) + d8).astype(F32)
        bp[:, d8 * 128 : (d8 + 1) * 128] = mm(byte[...], perm, 1, 0).astype(BF)
    hidt[...] = jnp.transpose(hidden).astype(BF)
    cg.wait()
    gp[...] = gp[...] + gq[...]
    half = pl.ds(pl.multiple_of(k * 384, 384), 384)
    cg2 = remote(gp.at[half], gn.at[half], gss.at[1], gsr.at[1], n2)
    cg2.start()

    is_a = x < 2
    slots = [jnp.where(is_a, ((z % 4) * 2 + 1 - lo) * 2 + q, 16 + 8 * (x - 2) + z) for q in range(2)]
    hi_d = jnp.where(is_a, x, 1 - lo)
    lo_d = (p + hi_d) % 2
    cores = [jnp.where(is_a, z // 4, q) for q in range(2)]
    per = CH // 2
    for q in range(2):
        for i in range(q * per, (q + 1) * per):
            cols = pl.ds(i * CW, CW)
            c2[i][0].wait_recv()
            c2[i][1].wait_recv()
            both = r2[0, :, cols].astype(F32) + r2[1, :, cols].astype(F32)
            for jj in range(CW // 128):
                j = (i * (CW // 128) + jj) % 8
                ft[q, pl.ds(j, 64, stride=8), :] = both[:, jj * 128 : (jj + 1) * 128]
        f[pl.ds(q * 32, 32)] = ft[q].astype(BF).reshape(32, 2, 8, 128)

        def send(i, _, q=q):
            x_, z_ = (x + i // 8) % 4, (z + i % 8) % 8
            same = (i == 0) & (hi_d == hi) & (cores[q] == k)

            @pl.when(jnp.logical_not(same))
            def _():
                remote(
                    f.at[q * 32 + x_ * 8 + z_], rx.at[k, :, slots[q]], r3s, r3r,
                    dev(x_, z_, lo_d, hi_d, cores[q]),
                ).start()

            return 0

        lax.fori_loop(0, 32, send, 0)
    mine = [(hi_d == hi) & (cores[q] == k) for q in range(2)]
    n_self = mine[0].astype(jnp.int32) + mine[1].astype(jnp.int32)
    for q in range(2):

        @pl.when(mine[q])
        def _(q=q):
            rx[k, :, slots[q]] = f[q * 32 + x * 8 + z]

    def wait_all(n_self, sem):
        for n in range(3):

            @pl.when(n_self == n)
            def _(n=n):
                piece = f.at[pl.ds(0, 64 - n)]
                pltpu.make_async_copy(piece, piece, sem).wait()

    wait_all(n_self, r3r)

    for c in range(4):
        at = jnp.transpose(rx[c // 2, c % 2, 0:16].astype(F32).reshape(128, 128))
        for d8 in range(8):
            la[c * 16 : (c + 1) * 16, d8 * 128 : (d8 + 1) * 128] = at[d8 * 16 : (d8 + 1) * 16].astype(BF)
        xf[c * 128 : (c + 1) * 128, :] = rx[c // 2, c % 2, 16:32].astype(F32).reshape(128, 128)
    for j in range(8):
        lb[:, j * 128 : (j + 1) * 128] = xf[pl.ds(j, 64, stride=8), :].astype(BF)
    pt = mm(la[...], bp[...], 1, 1)
    qt = mm(lb[...], outt[...], 1, 1)
    rt = mm(lb[...], byte[...], 1, 1)
    ss = mm(lb[...], lb[...], 1, 1)
    for c in range(4):
        rows = slice(c * 16, (c + 1) * 16)
        ms[c, 0:16, :] = pt[rows].astype(BF)
        ms[c, 16:32, :] = qt[rows].astype(BF)
        ms[c, 32:48, :] = rt[rows].astype(BF)
        ms[c, 48:64, :] = jnp.zeros((16, 256), BF)
        ms[c, 48:64, 0:16] = ss[rows, c * 16 : (c + 1) * 16].astype(BF)
    me = k * 2 + hi

    def member(o):
        k_, hi_ = (k + o // 2) % 2, (hi + o % 2) % 2
        return k_ * 2 + hi_, dev(x, z, (p + hi_) % 2, hi_, k_)

    ce = []
    for o in range(1, 4):
        c_, to = member(o)
        c = remote(ms.at[c_], er.at[o], e1s.at[o], e1r.at[o], to)
        c.start()
        ce.append(c)

    cg2.wait()
    cg3 = remote(gn.at[half], gn.at[half], gss.at[2], gsr.at[2], partner)
    cg3.start()
    tok_hot = (iota((256, 256), 0) == tok[...]).astype(F32)
    lab_hot = (iota((256, 256), 0) == lab[...]).astype(F32)
    ct = mm(lab_hot, tok_hot, 1, 1)
    cnt = jnp.sum(ct, 0, keepdims=True)
    cg3.wait()
    gram = gp[...] + gn[...]
    obt, oo, bbm = gram[0:256], gram[256:512], gram[512:768]
    diag = iota((256, 256), 0) == iota((256, 256), 1)
    bb = jnp.sum(jnp.where(diag, bbm, 0.0), 0, keepdims=True)
    scale = lax.rsqrt(bb * (1 / 4096) + EPS)
    own = ms[me].astype(F32)
    for c in ce:
        c.wait_recv()
    for o in range(1, 4):
        own = own + er[o].astype(F32)
    u, xx, yy, zz, loss = two_steps(
        own[0:16], own[16:32], own[32:48], own[48:64, 0:16], obt, oo, bbm, bb, scale, ct, cnt
    )
    loss_o[0] = loss * (1 / 256)
    cm[0:16, :] = u.astype(BF)
    cm[16:32, :] = xx.astype(BF)
    cm[32:48, :] = yy.astype(BF)
    cm[48:64, :] = jnp.zeros((16, 256), BF)
    cm[48:64, 0:16] = zz.astype(BF)
    cc = []
    for o in range(1, 4):
        _, to = member(o)
        c = remote(cm, cr.at[me], e2s.at[o], e2r.at[o], to)
        c.start()
        cc.append(c)
    cr[me] = cm[...]
    for c in cc:
        c.wait_recv()

    allc = cr[...]
    us = allc[:, 0:16].reshape(64, 256)
    xs = allc[:, 16:32].reshape(64, 256)
    ys = allc[:, 32:48].reshape(64, 256)
    dat = mm(us, bp[...], 1, 0)
    for c in range(4):
        for d8 in range(8):
            ta[d8 * 16 : (d8 + 1) * 16, :] = dat[c * 16 : (c + 1) * 16, d8 * 128 : (d8 + 1) * 128]
        tx[c // 2, c % 2, 0:16] = jnp.transpose(ta[...]).astype(BF).reshape(16, 8, 128)
    dbs = mm(xs, outt[...], 1, 0) + mm(ys, byte[...], 1, 0)
    zdb = [mm(cr[c, 48:64, 0:16], lb[c * 16 : (c + 1) * 16, :], 1, 0) for c in range(4)]
    dbs = dbs + jnp.concatenate(zdb, axis=0)
    for j in range(8):
        xf[pl.ds(j, 64, stride=8), :] = dbs[:, j * 128 : (j + 1) * 128]
    for c in range(4):
        tx[c // 2, c % 2, 16:32] = xf[c * 128 : (c + 1) * 128, :].astype(BF).reshape(16, 8, 128)

    spot = x * 8 + z

    def giver(s):
        if_a = s < 16
        b = s // 2
        r = s - 16
        x_ = jnp.where(if_a, hi, 2 + r // 8)
        z_ = jnp.where(if_a, k * 4 + b // 2, r % 8)
        lo_ = jnp.where(if_a, 1 - b % 2, 1 - hi)
        hi_ = (p + lo_) % 2
        q_ = jnp.where(if_a, s % 2, k)
        return x_, z_, lo_, hi_, q_

    def give(i, _):
        s, k_ = i // 2, i % 2
        x_, z_, lo_, hi_, q_ = giver(s)
        same = (x_ == x) & (z_ == z) & (hi_ == hi) & (k_ == k)

        @pl.when(jnp.logical_not(same))
        def _():
            remote(
                tx.at[k_, :, s], g_in.at[q_ * 32 + spot], r4s, r4r, dev(x_, z_, lo_, hi_, k_)
            ).start()

        return 0

    lax.fori_loop(0, 64, give, 0)
    for q in range(2):

        @pl.when(mine[q])
        def _(q=q):
            g_in[q * 32 + spot] = tx[k, :, slots[q]]

    wait_all(n_self, r4r)

    c5 = []
    for n, to in enumerate((n1, n2)):
        c = remote(g_in, d_in.at[k, p], r5s.at[n], r5r.at[n], to)
        c.start()
        c5.append(c)
    c6 = []
    for n in range(2):
        c5[n].wait_recv()
        from_p = (p + 1 + n) % 2
        c = remote(d_in.at[k, from_p], d_in.at[k, from_p], r6s.at[n], r6r.at[n], partner)
        c.start()
        c6.append(c)
    for n in range(2):
        c6[n].wait_recv()
    for kp in range(4):
        xd = d_in[kp // 2, kp % 2].astype(F32).reshape(1024, 128)
        ft[0] = xd[0:512]
        ft[1] = xd[512:1024]
        for j in range(16):
            dn[kp * 64 : (kp + 1) * 64, j * 128 : (j + 1) * 128] = ft[
                j // 8, pl.ds(j % 8, 64, stride=8), :
            ].astype(BF)

    for i in range(4):
        rows = slice(i * 256, (i + 1) * 256)
        hb[rows, :] = mm(w[rows, :], dn[...], 1, 1).astype(BF)
    ca = []
    for o in range(1, 8):
        x_, lo_ = (x + o // 2) % 4, (lo + o % 2) % 2
        rows = pl.ds(pl.multiple_of(x_ * 256 + lo_ * 128, 128), 128)
        c = remote(hb.at[rows], a1.at[o], p1s.at[o], p1r.at[o], dev(x_, z, lo_, hi, k))
        c.start()
        ca.append(c)
    base = pl.multiple_of(x * 256 + lo * 128, 128)
    acc = hb[pl.ds(base, 128), :].astype(F32)
    for o in range(1, 8):
        ca[o - 1].wait_recv()
        acc = acc + a1[o].astype(F32)
    a1s[...] = acc.astype(BF)
    cb = []
    for o in range(1, 8):
        z_ = (z + o) % 8
        c = remote(
            a1s.at[pl.ds(pl.multiple_of(z_ * 16, 16), 16)], a2.at[o], p2s.at[o], p2r.at[o],
            dev(x, z_, lo, hi, k),
        )
        c.start()
        cb.append(c)
    total = a1s[pl.ds(pl.multiple_of(z * 16, 16), 16), :].astype(F32)
    for o in range(1, 8):
        cb[o - 1].wait_recv()
        total = total + a2[o].astype(F32)
    row0 = pl.multiple_of(base + z * 16, 16)
    total = jnp.where(hidt[pl.ds(row0, 16), :].astype(F32) > 0, total, 0.0)
    big = total.astype(BF)
    small = (total - big.astype(F32)).astype(BF)
    piece = mm(big, chosen_s[...], 1, 0) + mm(small, chosen_s[...], 1, 0)
    ag[pl.ds(row0, 16), :] = piece.astype(BF)
    cd = []
    for o in range(1, 8):
        own_rows = ag.at[pl.ds(row0, 16)]
        c = remote(own_rows, own_rows, p3s.at[o], p3r.at[o], dev(x, (z + o) % 8, lo, hi, k))
        c.start()
        cd.append(c)
    for c in cd:
        c.wait_recv()
    cf = []
    for o in range(1, 8):
        x_, lo_ = (x + o // 2) % 4, (lo + o % 2) % 2
        own_rows = ag.at[pl.ds(base, 128)]
        c = remote(own_rows, own_rows, p4s.at[o], p4r.at[o], dev(x_, z, lo_, hi, k))
        c.start()
        cf.append(c)
    for c in cf:
        c.wait_recv()
    ing_o[...] = jnp.transpose(ag[...].astype(F32))

    for c in c1 + [c for ab in c2 for c in ab] + ce + cc + c5 + c6 + ca + cb + cd + cf:
        c.wait_send()
    wait_all(n_self, r3s)
    wait_all(n_self, r4s)


def local(client_ids, client_table, in_weight, in_bias, head_weight, tokens, labels, byte_table, out_table):
    vmem = pl.BlockSpec(memory_space=pltpu.VMEM)
    dma = pltpu.SemaphoreType.DMA
    V = pltpu.VMEM
    in_grad, dn, hid, losses = pl.pallas_call(
        kernel,
        out_shape=(
            jax.ShapeDtypeStruct((256, 1024), F32),
            jax.ShapeDtypeStruct((256, 2048), BF),
            jax.ShapeDtypeStruct((256, 1024), BF),
            jax.ShapeDtypeStruct((1,), F32),
        ),
        in_specs=[vmem] * 4 + [pl.BlockSpec(memory_space=pl.ANY)] + [vmem] * 4,
        out_specs=(vmem, vmem, vmem, pl.BlockSpec(memory_space=pltpu.SMEM)),
        scratch_shapes=[
            V((1024, 2048), BF),
            V((256, 2048), F32),
            V((128, 2048), F32),
            V((128, 2048), BF),
            V((2, 64, 2048), BF),
            V((2, 512, 128), F32),
            V((64, 2, 8, 128), BF),
            V((2, 2, 32, 8, 128), BF),
            V((64, 1024), BF),
            V((64, 1024), BF),
            V((512, 128), F32),
            V((256, 1024), BF),
            V((768, 256), F32),
            V((768, 256), F32),
            V((768, 256), F32),
            V((4, 64, 256), BF),
            V((4, 64, 256), BF),
            V((64, 256), BF),
            V((4, 64, 256), BF),
            V((128, 128), F32),
            V((2, 2, 32, 8, 128), BF),
            V((64, 2, 8, 128), BF),
            V((2, 2, 64, 2, 8, 128), BF),
            V((1024, 256), BF),
            V((8, 128, 256), BF),
            V((128, 256), BF),
            V((8, 16, 256), BF),
            V((1024, 256), BF),
            V((1024, 256), BF),
            V((256, 256), BF),
            dma((CH,)),
            dma((CH,)), dma((CH,)),
            dma((2, CH)), dma((2, CH)),
            dma((3,)), dma((3,)),
            dma(()), dma(()),
            dma((4,)), dma((4,)), dma((4,)), dma((4,)),
            dma(()), dma(()),
            dma((2,)), dma((2,)), dma((2,)), dma((2,)),
            dma((8,)), dma((8,)), dma((8,)), dma((8,)),
            dma((8,)), dma((8,)), dma((8,)), dma((8,)),
        ],
        compiler_params=pltpu.CompilerParams(
            collective_id=0, has_side_effects=True, vmem_limit_bytes=56 * 1024 * 1024
        ),
        name="round",
    )(
        client_ids.reshape(1, 256), client_table, in_weight, in_bias.reshape(1, 1024), head_weight,
        tokens, labels, byte_table, out_table,
    )
    head_grad = lax.dot_general(hid, dn, (((0,), (0,)), ((), ())), preferred_element_type=F32)
    return head_grad.astype(BF), in_grad, losses


def solution(mesh):
    placed = (
        P(),
        P(),
        P(None, "client"),
        P("client"),
        P("client", "head"),
        P(("head", "client"), None),
        P(("head", "client"), None),
        P(None, "client"),
        P(None, "client"),
    )
    return jax.shard_map(
        local,
        mesh=mesh,
        in_specs=placed,
        out_specs=(P("client", "head"), P(None, "client"), P(("head", "client"))),
        check_vma=False,
    )
```

time: 239 us -> 107 us (0.45); the launches traced: 235 us -> 106 us
  blocking collectives: 132 us -> 0 us
  Pallas kernels: 0 us -> 97.5 us
  matrix products: 46.4 us -> 4.78 us
  between operations: 16.5 us -> 2.34 us
  waiting for transfers between devices: 12.3 us -> 0 us
  local copies, waits for them, and re-layouts: 12.1 us -> 0.97 us
  other arithmetic: 8.39 us -> 0 us
  starting transfers between devices: 6.88 us -> 0 us
    all_to_all x5 -> x0, blocking collectives: 132 us -> none  [the longest x1 49.5 us: summed_on_arrival(): lax.all_to_all(pieces, axis, split_axis=0, concat_axis=0, tiled=True)]
    pallas_call x0 -> x1, Pallas kernels: none -> 97.5 us  [local(): pl.pallas_call(kernel, out_shape=(jax.ShapeDtypeStruct((256, 1024), F32),...]
    dot_general x20 -> x1, matrix products: 46.4 us -> 4.78 us  [local(): lax.dot_general(hid, dn, (((0,), (0,)), ((), ())), preferred_element_type...]
    all_to_all x1 -> x0, waiting for transfers between devices: 12.3 us -> none  [sent_to_all(): return lax.all_to_all(copies, axis, split_axis=0, concat_axis=0, tiled=True)]
    all_to_all x1 -> x0, starting transfers between devices: 6.84 us -> none  [sent_to_all(): return lax.all_to_all(copies, axis, split_axis=0, concat_axis=0, tiled=True)]
    reshape x6 -> x0, local copies, waits for them, and re-layouts: 3.05 us -> none  [the longest x2 1.14 us: train_client(): factor_row[:split_at].reshape(depth, rank_size).astype(jnp.float32)]
    reduce_sum x5 -> x0, other arithmetic: 2.82 us -> none  [the longest x1 1.8 us: summed_on_arrival(): return arrived.sum(axis=0)]
    unnamed x1 -> x0, other arithmetic: 2.41 us -> none
  transfers between devices with their start and end apart: 2 -> 0, of which waited for: 1 -> 0; matrix products, arithmetic and copies ran while one was open for 7% -> 0% of each run, Pallas kernels for 0% -> 0%
where the time goes in v1:
time: 107 us; the launch traced here: 106 us
  Pallas kernels  97.5 us (91%)
  matrix products  4.78 us (4%)
  between operations  2.34 us (2%)
    pallas_call x1, Pallas kernels, local(): pl.pallas_call(kernel, out_shape=(jax.ShapeDtypeStruct((256, 1024), F32),...  97.5 us
    dot_general x1, matrix products, local(): lax.dot_general(hid, dn, (((0,), (0,)), ((), ())), preferred_element_type...  4.78 us

profile of v1, /device:TPU:2, one launch (start us, length us, event | category | flops | bytes accessed | tf_op | source)
XLA Modules:
  0.0 105.6 jit_solution(11769050782935317513)
XLA Ops:
  0.6 97.5 %round.1 = (f32[256,1024]{1,0:T(8,128)}, bf16[256,2048]{1,0:T(8,128)(2,1)}, bf16[256,1024]{1,0:T(8,128)(2,1)}, f32[1]{0:T(128)}) custom-call(s32[1,256]{1,0:T(1,128)} %bitcast.5, bf16[1024,256]{1,0:T(8,128)(2,1)} %table.1, bf16[256,1024]{1,0:T(8,128)(2,1)} %inw.1, f32[1,1024]{1,0:T(1,128)} %bitcast.4, bf16[1024,2048]{1,0:T(8,128)(2,1)} %w_hbm.1, ...), custom_call_target="tpu_custom_call" | custom-call | tf_op jit(solution)/shard_map/round/pallas_call | solution.py:437
  98.1 0.0 copy-start
  98.1 4.8 %convolution_convert_fusion = bf16[1024,2048]{1,0:T(8,128)(2,1)} fusion(bf16[256,1024]{1,0:T(8,128)(2,1)} %get-tuple-element.7, bf16[256,2048]{1,0:T(8,128)(2,1)} %get-tuple-element.8), kind=kOutput, calls=%fused_computation | convolution fusion | flops 1075838976 | bytes 5767168 | tf_op jit(solution)/shard_map/dot_general | solution.py:497
  102.9 0.0 copy-done
  102.9 1.0 copy.14
Async XLA Ops:
  98.1 4.8 %copy-start = (f32[256,1024]{1,0:T(8,128)S(1)}, f32[256,1024]{1,0:T(8,128)}, u32[]{:S(2)}) copy-start(f32[256,1024]{1,0:T(8,128)} %get-tuple-element.15) | copy-start | bytes 3145732

commit v2 on v1

v2 whole, which is shorter than its diff:
```python
import jax
import jax.numpy as jnp
from jax import lax
from jax.experimental import pallas as pl
from jax.experimental.pallas import tpu as pltpu
from jax.sharding import PartitionSpec as P

EPS = 1e-6
ETA = 0.1
F32 = jnp.float32
BF = jnp.bfloat16
MESH = pl.DeviceIdType.MESH
CH = 4
CW = 2048 // CH


def mm(a, b, ca, cb):
    return lax.dot_general(
        a.astype(BF), b.astype(BF), (((ca,), (cb,)), ((), ())), preferred_element_type=F32
    )


def iota(shape, dim):
    return lax.broadcasted_iota(jnp.int32, shape, dim)


def gradients(pt, qt, rt, s_mat, obt, bb, scale, ct, cnt):
    tt = pt * (scale * (1 / 256))
    st = mm(s_mat, tt, 1, 0)
    msq = (bb + jnp.sum(tt * (2 * rt + st), 0, keepdims=True)) * (1 / 4096)
    q = lax.rsqrt(msq + EPS)
    mt = obt + mm(qt, tt, 0, 0)
    lg = mt * (q * (1 / 16))
    top = jnp.max(lg, 0, keepdims=True)
    ex = jnp.exp(lg - top)
    total = jnp.sum(ex, 0, keepdims=True)
    gt = (ex * (cnt / total) - ct) * (1 / 16)
    along = jnp.sum(gt * mt, 0, keepdims=True)
    e = q * q * q * along * (1 / 4096)
    ht = gt * q
    dt = mm(qt, ht, 1, 0) - e * (rt + st)
    ut = dt * (scale * (1 / 256))
    xt = mm(tt, ht, 1, 1)
    yt = tt * e
    z = mm(yt, tt, 1, 1)
    loss = jnp.sum(cnt * (top + jnp.log(total)) - jnp.sum(ct * lg, 0, keepdims=True))
    return ut, xt, yt, z, loss


def two_steps(pt, qt, rt, s_mat, obt, oo, bbm, bb, scale, ct, cnt):
    u1, x1, y1, z1, loss = gradients(pt, qt, rt, s_mat, obt, bb, scale, ct, cnt)
    vo = -ETA * mm(x1, oo, 1, 0) + ETA * mm(y1, obt, 1, 1)
    vb = -ETA * mm(x1, obt, 1, 0) + ETA * mm(y1, bbm, 1, 0)
    z1 = ETA * z1
    p2 = pt - ETA * mm(u1, bbm, 1, 0)
    q2 = qt + mm(z1, qt, 1, 0) + vo
    r2 = rt + mm(z1, rt, 1, 0) + vb
    h = -ETA * mm(qt, x1, 1, 1) + ETA * mm(rt, y1, 1, 1)
    ht = -ETA * mm(x1, qt, 1, 1) + ETA * mm(y1, rt, 1, 1)
    vv = -ETA * mm(x1, vo, 1, 1) + ETA * mm(y1, vb, 1, 1)
    zs = mm(z1, s_mat, 1, 0)
    s2 = s_mat + zs + mm(s_mat, z1, 1, 1) + mm(zs, z1, 1, 1)
    s2 = s2 + h + mm(z1, h, 1, 0) + ht + mm(ht, z1, 1, 1) + vv
    u2, x2, y2, z2, _ = gradients(p2, q2, r2, s2, obt, bb, scale, ct, cnt)
    z2 = ETA * z2
    u = -ETA * (u1 + u2)
    x = -ETA * (x1 + mm(z2, x1, 1, 0) + x2)
    y = ETA * (y1 + mm(z2, y1, 1, 0) + y2)
    z = z1 + z2 + mm(z2, z1, 1, 0)
    return u, x, y, z, loss

def tail_kernel(hidt, dn, ag, hg_o, ing_o, hv, dv, av, gv, iv, sem, osem):
    cols = [pl.ds(i * 512, 512) for i in range(4)]
    loads = [pltpu.make_async_copy(hidt, hv, sem.at[0])]
    loads += [pltpu.make_async_copy(dn.at[:, cols[i]], dv.at[:, cols[i]], sem.at[1 + i]) for i in range(4)]
    loads.append(pltpu.make_async_copy(ag, av, sem.at[5]))
    for c in loads:
        c.start()
    loads[0].wait()
    outs = []
    for i in range(4):
        loads[1 + i].wait()
        gv[:, cols[i]] = jnp.dot(hv[...], dv[:, cols[i]], preferred_element_type=F32).astype(BF)
        outs.append(pltpu.make_async_copy(gv.at[:, cols[i]], hg_o.at[:, cols[i]], osem.at[i]))
        outs[-1].start()
        if i == 2:
            loads[5].wait()
            iv[...] = jnp.transpose(av[...].astype(F32))
            outs.append(pltpu.make_async_copy(iv, ing_o, osem.at[4]))
            outs[-1].start()
    for c in outs:
        c.wait()


FAR = (4, 3, 5, 2, 6, 1, 7, 0)
FAR_X = (2, 1, 3, 0)
BACK = (0, 1, 7, 4, 3, 5, 2, 6)
SOON = (0, 1, 7, 2, 6, 3, 5, 4)


def kernel(
    ids_h, table_h, inw_h, bias_h, w_hbm, tok_h, lab_h, byte_h, outt_h,
    ag_o, dn_o, hidt_o, loss_o,
    ids, bias, tok, lab, table, inw, byte, outt,
    w, hid, fs, fr, sb, r2, ft, f, rx, la, lb, xf, bp, gp, gq, ga, gb, na, nb, ms, er, cm, cr, ta, tx, g_in,
    d_in, dn, hb, a1, a1s, a2, ag, hidt, chosen_s, like,
    sl, sw, so, r1s, r1r, r2s, r2r, gs, gr, r3s, r3r, e1s, e1r, e2s, e2r, r4s, r4r, r5s, r5r, r6s, r6r,
    p1s, p1r, p2s, p2r, p3s, p3r, p4s, p4r,
):
    rem, div = lax.rem, lax.div
    head = lax.axis_index("head")
    grp = lax.axis_index("client")
    x, z, lo = div(head, 16), rem(div(head, 2), 8), rem(head, 2)
    hi, k = div(grp, 2), rem(grp, 2)
    p = rem(hi + lo, 2)
    xs = [rem(x + d, 4) for d in range(4)]
    zs = [rem(z + d, 8) for d in range(8)]
    ks = [k, 1 - k]
    his = [hi, 1 - hi]
    los = [lo, 1 - lo]
    xz16 = [[xs[dx] * 16 + zs[dz] * 2 for dz in range(8)] for dx in range(4)]

    def remote(src, dst, ss, rs, to):
        return pltpu.make_async_remote_copy(
            src_ref=src, dst_ref=dst, send_sem=ss, recv_sem=rs, device_id=to, device_id_type=MESH
        )

    def drain(like_ref, sem):
        pltpu.make_async_copy(like_ref, like_ref, sem).wait()

    partner = (head, hi * 2 + 1 - k)
    n1 = (xz16[0][0] + 1 - lo, grp)
    n2 = (xz16[0][0] + 1 - lo, (1 - hi) * 2 + k)

    ins = [
        pltpu.make_async_copy(src, dst, sl.at[i])
        for i, (src, dst) in enumerate(
            (
                (ids_h, ids), (table_h, table), (bias_h, bias), (inw_h, inw),
                (byte_h, byte), (outt_h, outt), (tok_h, tok), (lab_h, lab),
            )
        )
    ]
    wc = [
        pltpu.make_async_copy(w_hbm.at[:, pl.ds(i * CW, CW)], w.at[:, pl.ds(i * CW, CW)], sw.at[i])
        for i in range(CH)
    ]
    for c in ins[:4] + wc + ins[4:]:
        c.start()

    bar = pltpu.get_barrier_semaphore()
    for dz in FAR:
        for dx in FAR_X:
            for dh in range(2):
                for dk in range(2):
                    if dx or dz or dh or dk:
                        to = (xz16[dx][dz] + los[dh], his[dh] * 2 + ks[dk])
                        pl.semaphore_signal(bar, inc=1, device_id=to, device_id_type=MESH)
    for dx in range(4):
        pl.semaphore_signal(bar, inc=1, device_id=(xz16[dx][0] + 1 - lo, grp), device_id_type=MESH)

    m = iota((256, 256), 1)
    mhi, mx, mz, mp, mk = m % 2, (m // 2) % 4, (m // 8) % 8, (m // 64) % 2, m // 128
    owner = (mx * 16 + mz * 2 + (mp + mhi) % 2) * 4 + mhi * 2 + mk
    order = (iota((256, 256), 0) == owner).astype(BF)
    ins[0].wait()
    picks = (iota((1024, 256), 0) == ids[...]).astype(F32).astype(BF)
    picks = mm(picks, order, 1, 0)
    ins[1].wait()
    chosen = mm(picks, table[...], 0, 0).astype(BF)
    chosen_s[...] = chosen
    ins[2].wait()
    ins[3].wait()
    pre = mm(chosen, inw[...], 1, 0) + bias[...]
    hidden = jnp.maximum(pre, 0.0)
    hid[...] = hidden.astype(BF)

    for i in range(CH):
        cols = pl.ds(i * CW, CW)
        wc[i].wait()
        fs[:, :, :, :, cols] = jnp.dot(hid[...], w[:, cols], preferred_element_type=F32).reshape(
            2, 2, 8, 8, CW
        )

    pl.semaphore_wait(bar, 131)

    c1 = []
    for dz in FAR:
        c = remote(fs.at[1 - k, :, zs[dz]], fr.at[:, zs[dz]], r1s, r1r.at[dz], partner)
        c.start()
        c1.append(c)
    ins[4].wait()
    ins[5].wait()
    gp[0:256, :] = mm(outt[...], byte[...], 1, 1)
    gp[256:512, :] = mm(outt[...], outt[...], 1, 1)
    gp[512:768, :] = mm(byte[...], byte[...], 1, 1)
    cg = remote(gp, gq, gs.at[0], gr.at[0], partner)
    cg.start()
    diag = iota((256, 256), 0) == iota((256, 256), 1)
    ra = pl.ds(pl.multiple_of(k * 160 + x * 40, 8), 40)
    rb = pl.ds(pl.multiple_of(k * 256 + x * 64, 64), 64)
    cg2 = [
        remote(ga.at[ra], na.at[ra], gs.at[1], gr.at[1], n2),
        remote(gb.at[rb], nb.at[rb], gs.at[2], gr.at[2], n2),
    ]
    for i, dz in enumerate(FAR):
        c1[i].wait_recv()
        sb[:, zs[dz]] = (fs[k, :, zs[dz]] + fr[:, zs[dz]]).astype(BF)
        remote(sb.at[1 - p, zs[dz]], r2.at[0, zs[dz]], r2s, r2r.at[dz], n1).start()
        remote(sb.at[p, zs[dz]], r2.at[1, zs[dz]], r2s, r2r.at[dz], n2).start()
        if i == 5:
            cg.wait_recv()
            gsum = gp[...] + gq[...]
            ga[0:256, :] = gsum[0:256]
            ga[256:320, :] = jnp.broadcast_to(
                jnp.sum(jnp.where(diag, gsum[512:768], 0.0), 0, keepdims=True), (64, 256)
            )
            gb[...] = gsum[256:768].astype(BF)
            for c in cg2:
                c.start()

    for d8 in range(8):
        perm = (iota((1024, 128), 0) == 8 * iota((1024, 128), 1) + d8).astype(F32)
        bp[:, d8 * 128 : (d8 + 1) * 128] = mm(byte[...], perm, 1, 0).astype(BF)
    ins[6].wait()
    ins[7].wait()
    tok_hot = (iota((256, 256), 0) == tok[...]).astype(F32)
    lab_hot = (iota((256, 256), 0) == lab[...]).astype(F32)
    ct = mm(lab_hot, tok_hot, 1, 1)
    cnt = jnp.sum(ct, 0, keepdims=True)
    hidt[...] = jnp.transpose(hid[...].astype(F32)).astype(BF)
    co = [pltpu.make_async_copy(hidt, hidt_o, so.at[0])]
    co[0].start()

    is_a = x < 2
    slots = [jnp.where(is_a, (rem(z, 4) * 2 + 1 - lo) * 2 + q, 16 + 8 * (x - 2) + z) for q in range(2)]
    hi_d = jnp.where(is_a, x, 1 - lo)
    lo_d = rem(p + hi_d, 2)
    cores = [jnp.where(is_a, div(z, 4), q) for q in range(2)]
    to_c = [hi_d * 2 + cores[q] for q in range(2)]
    mine = [to_c[q] == grp for q in range(2)]
    n_self = mine[0].astype(jnp.int32) + mine[1].astype(jnp.int32)
    for i, dz in enumerate(FAR):
        drain(r2.at[:, zs[dz]], r2r.at[dz])
        both = r2[0, zs[dz]].astype(F32) + r2[1, zs[dz]].astype(F32)
        for q in range(2):
            for j in range(8):
                at = (q * 8 + j) * 128
                ft[q, pl.ds(j, 8, stride=8), :] = both[:, at : at + 128]
            f[q, zs[dz]] = ft[q, 0:64].astype(BF).reshape(4, 2, 8, 128)
        for dx in FAR_X:
            for q in range(2):
                c = remote(
                    f.at[q, zs[dz], xs[dx]], rx.at[k, :, slots[q]], r3s, r3r, (xz16[dx][dz] + lo_d, to_c[q])
                )
                if dz or dx:
                    c.start()
                else:
                    pl.when(jnp.logical_not(mine[q]))(c.start)
        if i == 6:
            for c in cg2:
                c.wait_recv()
            for dx in (2, 1, 3):
                to = (xz16[dx][0] + lo, grp)
                remote(na.at[ra], na.at[ra], gs.at[1], gr.at[3], to).start()
                remote(nb.at[rb], nb.at[rb], gs.at[2], gr.at[4], to).start()
    for q in range(2):

        @pl.when(mine[q])
        def _(q=q):
            rx[k, :, slots[q]] = f[q, z, x]

    def wait_all(sem):
        for n in range(3):

            @pl.when(n_self == n)
            def _(n=n):
                piece = like.at[pl.ds(0, 64 - n)]
                pltpu.make_async_copy(piece, piece, sem).wait()

    wait_all(r3r)

    drain(na.at[pl.ds(0, 120)], gr.at[3])
    drain(nb.at[pl.ds(0, 192)], gr.at[4])
    ha = pl.ds(pl.multiple_of(k * 160, 8), 160)
    hbb = pl.ds(pl.multiple_of(k * 256, 256), 256)
    cg3 = [
        remote(na.at[ha], na.at[ha], gs.at[1], gr.at[5], partner),
        remote(nb.at[hbb], nb.at[hbb], gs.at[2], gr.at[6], partner),
    ]
    for c in cg3:
        c.start()
    for c in range(4):
        at = jnp.transpose(rx[c // 2, c % 2, 0:16].astype(F32).reshape(128, 128))
        for d8 in range(8):
            la[c * 16 : (c + 1) * 16, d8 * 128 : (d8 + 1) * 128] = at[d8 * 16 : (d8 + 1) * 16].astype(BF)
        xf[c * 128 : (c + 1) * 128, :] = rx[c // 2, c % 2, 16:32].astype(F32).reshape(128, 128)
    for j in range(8):
        lb[:, j * 128 : (j + 1) * 128] = xf[pl.ds(j, 64, stride=8), :].astype(BF)
    pt = mm(la[...], bp[...], 1, 1)
    qt = mm(lb[...], outt[...], 1, 1)
    rt = mm(lb[...], byte[...], 1, 1)
    ss = mm(lb[...], lb[...], 1, 1)
    for c in range(4):
        rows = slice(c * 16, (c + 1) * 16)
        ms[c, 0:16, :] = pt[rows].astype(BF)
        ms[c, 16:32, :] = qt[rows].astype(BF)
        ms[c, 32:48, :] = rt[rows].astype(BF)
        ms[c, 48:64, :] = jnp.zeros((16, 256), BF)
        ms[c, 48:64, 0:16] = ss[rows, c * 16 : (c + 1) * 16].astype(BF)
    me = k * 2 + hi
    members = [
        (ks[o // 2] * 2 + his[o % 2], (xz16[0][0] + los[o % 2], his[o % 2] * 2 + ks[o // 2]))
        for o in range(4)
    ]
    for o in range(1, 4):
        c_, to = members[o]
        remote(ms.at[c_], er.at[o], e1s, e1r, to).start()
    for c in cg3:
        c.wait_recv()
    obt = ga[0:256, :] + na[0:256, :]
    bb = ga[256:257, :] + na[256:257, :]
    grams = gb[...].astype(F32) + nb[...].astype(F32)
    oo, bbm = grams[0:256].astype(BF), grams[256:512].astype(BF)
    scale = lax.rsqrt(bb * (1 / 4096) + EPS)
    own = ms[me].astype(F32)
    drain(er.at[pl.ds(1, 3)], e1r)
    for o in range(1, 4):
        own = own + er[o].astype(F32)
    u, xx, yy, zz, loss = two_steps(
        own[0:16], own[16:32], own[32:48], own[48:64, 0:16], obt, oo, bbm, bb, scale, ct, cnt
    )
    loss_o[0] = loss * (1 / 256)
    cm[0:16, :] = u.astype(BF)
    cm[16:32, :] = xx.astype(BF)
    cm[32:48, :] = yy.astype(BF)
    cm[48:64, :] = jnp.zeros((16, 256), BF)
    cm[48:64, 0:16] = zz.astype(BF)
    for o in range(1, 4):
        remote(cm, cr.at[me], e2s, e2r, members[o][1]).start()
    cr[me] = cm[...]
    drain(er.at[pl.ds(1, 3)], e2r)

    allc = cr[...]
    us = allc[:, 0:16].reshape(64, 256)
    xc = allc[:, 16:32].reshape(64, 256)
    yc = allc[:, 32:48].reshape(64, 256)
    dat = mm(us, bp[...], 1, 0)
    for c in range(4):
        for d8 in range(8):
            ta[d8 * 16 : (d8 + 1) * 16, :] = dat[c * 16 : (c + 1) * 16, d8 * 128 : (d8 + 1) * 128]
        tx[c // 2, c % 2, 0:16] = jnp.transpose(ta[...]).astype(BF).reshape(16, 8, 128)
    dbs = mm(xc, outt[...], 1, 0) + mm(yc, byte[...], 1, 0)
    zdb = [mm(cr[c, 48:64, 0:16], lb[c * 16 : (c + 1) * 16, :], 1, 0) for c in range(4)]
    dbs = dbs + jnp.concatenate(zdb, axis=0)
    for j in range(8):
        xf[pl.ds(j, 64, stride=8), :] = dbs[:, j * 128 : (j + 1) * 128]
    for c in range(4):
        tx[c // 2, c % 2, 16:32] = xf[c * 128 : (c + 1) * 128, :].astype(BF).reshape(16, 8, 128)

    def give(slot, k_, q_, to, back, near):
        c = remote(tx.at[k_, :, slot], g_in.at[q_, z, x], r4s, r4r.at[back], to)
        if near:
            pl.when(jnp.logical_not((to[0] == head) & (to[1] == grp)))(c.start)
        else:
            c.start()

    z4 = [rem(z + d, 4) for d in (0, 1, 3, 2)]
    his_a = [rem(p + 1 - par, 2) for par in range(2)]
    for step in range(8):
        dz = BACK[step]
        for xh in range(2):
            for dk in range(2):
                slot = 16 + xh * 8 + zs[dz]
                to = (32 + xh * 16 + zs[dz] * 2 + 1 - hi, (1 - lo) * 2 + ks[dk])
                give(slot, ks[dk], k, to, (8 - dz) % 8, dz == 0)
        zr = z4[step // 2]
        za = k * 4 + zr
        back = rem(z - za + 8, 8)
        par = step % 2
        for q in range(2):
            for dk in range(2):
                slot = (zr * 2 + par) * 2 + q
                to = (hi * 16 + za * 2 + 1 - par, his_a[par] * 2 + ks[dk])
                give(slot, ks[dk], q, to, back, step // 2 == 0)
    for q in range(2):

        @pl.when(mine[q])
        def _(q=q):
            g_in[q, z, x] = tx[k, :, slots[q]]

    for dz in SOON:
        if dz:
            drain(like.at[pl.ds(0, 8)], r4r.at[dz])
        else:
            for n in range(3):

                @pl.when(n_self == n)
                def _(n=n):
                    drain(like.at[pl.ds(0, 8 - n)], r4r.at[0])

        for to in (n1, n2):
            remote(g_in.at[:, zs[dz]], d_in.at[k, p, :, zs[dz]], r5s, r5r.at[dz], to).start()
    for dz in SOON:
        drain(d_in.at[k, :, :, zs[dz]], r5r.at[dz])
        region = d_in.at[k, :, :, zs[dz]]
        remote(region, region, r6s, r6r, partner).start()
    drain(d_in.at[1 - k], r6r)
    for kp in range(4):
        xd = d_in[kp // 2, kp % 2].astype(F32).reshape(1024, 128)
        ft[0] = xd[0:512]
        ft[1] = xd[512:1024]
        for j in range(16):
            dn[kp * 64 : (kp + 1) * 64, j * 128 : (j + 1) * 128] = ft[
                j // 8, pl.ds(j % 8, 64, stride=8), :
            ].astype(BF)
    co.append(pltpu.make_async_copy(dn, dn_o, so.at[1]))
    co[1].start()

    turn = [rem(zn - z + 14, 8) * 16 for zn in range(8)]
    for i in range(4):
        part = mm(w[i * 256 : (i + 1) * 256, :], dn[...], 1, 1).astype(BF)
        for l_ in range(2):
            for zn in range(8):
                at = l_ * 128 + zn * 16
                hb[i, l_, pl.ds(pl.multiple_of(turn[zn], 16), 16), :] = part[at : at + 16]
    peers = [(xs[o // 2], los[o % 2], (xz16[o // 2][0] + los[o % 2], grp)) for o in range(8)]
    for h in range(2):
        rows = pl.ds(h * 64, 64)
        for o in (4, 5, 2, 3, 6, 7, 1):
            x_, lo_, to = peers[o]
            remote(hb.at[x_, lo_, rows], a1.at[o, rows], p1s, p1r.at[h], to).start()
    for h in range(2):
        rows = pl.ds(h * 64, 64)
        acc = hb[x, lo, rows, :].astype(F32)
        drain(a1.at[pl.ds(1, 7), rows], p1r.at[h])
        for o in range(1, 8):
            acc = acc + a1[o, rows, :].astype(F32)
        a1s[rows, :] = acc.astype(BF)
        for t in ((2, 1, 3, 0), (4, 7, 5, 6))[h]:
            dz = (t + 2) % 8
            if dz:
                remote(a1s.at[pl.ds(t * 16, 16)], a2.at[dz], p2s, p2r, (xz16[0][dz] + lo, grp)).start()
    total = a1s[96:112, :].astype(F32)
    drain(a2.at[pl.ds(1, 7)], p2r)
    for dz in range(1, 8):
        total = total + a2[dz].astype(F32)
    base = pl.multiple_of(x * 256 + lo * 128, 128)
    row0 = pl.multiple_of(base + z * 16, 16)
    total = jnp.where(hidt[pl.ds(row0, 16), :].astype(F32) > 0, total, 0.0)
    big = total.astype(BF)
    small = (total - big.astype(F32)).astype(BF)
    piece = mm(big, chosen_s[...], 1, 0) + mm(small, chosen_s[...], 1, 0)
    ag[pl.ds(row0, 16), :] = piece.astype(BF)
    cd = {}
    own_rows = ag.at[pl.ds(row0, 16)]
    for dz in FAR[:7]:
        cd[dz] = remote(own_rows, own_rows, p3s, p3r.at[dz], (xz16[0][dz] + lo, grp))
        cd[dz].start()
    for dz in (0, 1, 7, 2, 6, 3, 5, 4):
        if dz:
            cd[dz].wait_recv()
        rows = ag.at[pl.ds(pl.multiple_of(base + zs[(8 - dz) % 8] * 16, 16), 16)]
        for o in (4, 5, 2, 3, 6, 7, 1):
            remote(rows, rows, p4s, p4r, peers[o][2]).start()
    drain(a1.at[pl.ds(1, 7)], p4r)
    co.append(pltpu.make_async_copy(ag, ag_o, so.at[2]))
    co[2].start()

    drain(fr, r1s)
    drain(r2, r2s)
    drain(gq, gs.at[0])
    drain(na, gs.at[1])
    drain(nb, gs.at[2])
    drain(er.at[pl.ds(1, 3)], e1s)
    drain(er.at[pl.ds(1, 3)], e2s)
    drain(d_in.at[0], r5s)
    drain(d_in.at[0], r6s)
    drain(a1.at[pl.ds(1, 7)], p1s)
    drain(a2.at[pl.ds(1, 7)], p2s)
    drain(a2.at[pl.ds(1, 7)], p3s)
    drain(a1.at[pl.ds(1, 7)], p4s)
    wait_all(r3s)
    wait_all(r4s)
    for c in co:
        c.wait()


def local(client_ids, client_table, in_weight, in_bias, head_weight, tokens, labels, byte_table, out_table):
    hbm = pl.BlockSpec(memory_space=pl.ANY)
    dma = pltpu.SemaphoreType.DMA
    V = pltpu.VMEM
    S = jax.ShapeDtypeStruct
    ag, dn, hidt, losses = pl.pallas_call(
        kernel,
        out_shape=(S((1024, 256), BF), S((256, 2048), BF), S((1024, 256), BF), S((1,), F32)),
        in_specs=[hbm] * 9,
        out_specs=(hbm, hbm, hbm, pl.BlockSpec(memory_space=pltpu.SMEM)),
        scratch_shapes=[
            V((1, 256), jnp.int32),
            V((1, 1024), F32),
            V((1, 256), jnp.int32),
            V((1, 256), jnp.int32),
            V((1024, 256), BF),
            V((256, 1024), BF),
            V((256, 1024), BF),
            V((256, 1024), BF),
            V((1024, 2048), BF),
            V((256, 1024), BF),
            V((2, 2, 8, 8, 2048), F32),
            V((2, 8, 8, 2048), F32),
            V((2, 8, 8, 2048), BF),
            V((2, 8, 8, 2048), BF),
            V((2, 512, 128), F32),
            V((2, 8, 4, 2, 8, 128), BF),
            V((2, 2, 32, 8, 128), BF),
            V((64, 1024), BF),
            V((64, 1024), BF),
            V((512, 128), F32),
            V((256, 1024), BF),
            V((768, 256), F32),
            V((768, 256), F32),
            V((320, 256), F32),
            V((512, 256), BF),
            V((320, 256), F32),
            V((512, 256), BF),
            V((4, 64, 256), BF),
            V((4, 64, 256), BF),
            V((64, 256), BF),
            V((4, 64, 256), BF),
            V((128, 128), F32),
            V((2, 2, 32, 8, 128), BF),
            V((2, 8, 4, 2, 8, 128), BF),
            V((2, 2, 2, 8, 4, 2, 8, 128), BF),
            V((256, 2048), BF),
            V((4, 2, 128, 256), BF),
            V((8, 128, 256), BF),
            V((128, 256), BF),
            V((8, 16, 256), BF),
            V((1024, 256), BF),
            V((1024, 256), BF),
            V((256, 256), BF),
            V((64, 2, 8, 128), BF),
            dma((8,)), dma((CH,)), dma((3,)),
            dma(()), dma((8,)),
            dma(()), dma((8,)),
            dma((3,)), dma((7,)),
            dma(()), dma(()),
            dma(()), dma(()), dma(()), dma(()),
            dma(()), dma((8,)),
            dma(()), dma((8,)), dma(()), dma(()),
            dma(()), dma((2,)), dma(()), dma(()),
            dma(()), dma((8,)), dma(()), dma(()),
        ],
        compiler_params=pltpu.CompilerParams(
            collective_id=0, has_side_effects=True, vmem_limit_bytes=60 * 1024 * 1024
        ),
        name="round",
    )(
        client_ids.reshape(1, 256), client_table, in_weight, in_bias.reshape(1, 1024), head_weight,
        tokens, labels, byte_table, out_table,
    )
    head_grad, in_grad = pl.pallas_call(
        tail_kernel,
        out_shape=(S((1024, 2048), BF), S((256, 1024), F32)),
        in_specs=[hbm] * 3,
        out_specs=(hbm, hbm),
        scratch_shapes=[
            V((1024, 256), BF), V((256, 2048), BF), V((1024, 256), BF),
            V((1024, 2048), BF), V((256, 1024), F32),
            dma((6,)), dma((5,)),
        ],
        compiler_params=pltpu.CompilerParams(vmem_limit_bytes=60 * 1024 * 1024),
        name="tail",
    )(hidt, dn, ag)
    return head_grad, in_grad, losses


def solution(mesh):
    placed = (
        P(),
        P(),
        P(None, "client"),
        P("client"),
        P("client", "head"),
        P(("head", "client"), None),
        P(("head", "client"), None),
        P(None, "client"),
        P(None, "client"),
    )
    return jax.shard_map(
        local,
        mesh=mesh,
        in_specs=placed,
        out_specs=(P("client", "head"), P(None, "client"), P(("head", "client"))),
        check_vma=False,
    )
```

time: 107 us -> 89 us (0.83); the launches traced: 106 us -> 88.9 us
  Pallas kernels: 97.5 us -> 86.5 us
  matrix products: 4.78 us -> 0 us
    pallas_call x1 -> x2, Pallas kernels: 97.5 us -> 86.5 us  [the longest x1 82.4 us: local(): pl.pallas_call(kernel, out_shape=(S((1024, 256), BF), S((256, 2048), BF),...]
    dot_general x1 -> x0, matrix products: 4.78 us -> none  [local(): lax.dot_general(hid, dn, (((0,), (0,)), ((), ())), preferred_element_type...]
where the time goes in v2:
time: 89 us; the launch traced here: 88.9 us
  Pallas kernels  86.5 us (97%)
  between operations  2.39 us (3%)
    pallas_call x1, Pallas kernels, local(): pl.pallas_call(kernel, out_shape=(S((1024, 256), BF), S((256, 2048), BF),...  82.4 us
    pallas_call x1, Pallas kernels, local(): pl.pallas_call(tail_kernel, out_shape=(S((1024, 2048), BF), S((256, 1024)...  4.17 us

profile of v2, /device:TPU:2, one launch (start us, length us, event | category | flops | bytes accessed | tf_op | source)
XLA Modules:
  0.0 88.9 jit_solution(17813508583664116870)
XLA Ops:
  0.6 82.4 %round.1 = (bf16[1024,256]{1,0:T(8,128)(2,1)}, bf16[256,2048]{1,0:T(8,128)(2,1)}, bf16[1024,256]{1,0:T(8,128)(2,1)}, f32[1]{0:T(128)}) custom-call(s32[1,256]{1,0:T(1,128)} %bitcast.3, bf16[1024,256]{1,0:T(8,128)(2,1)} %table_h.1, bf16[256,1024]{1,0:T(8,128)(2,1)} %inw_h.1, f32[1,1024]{1,0:T(1,128)} %bitcast.2, bf16[1024,2048]{1,0:T(8,128)(2,1)} %w_hbm.1, ...), custom_call_target="tpu_custom_call" | custom-call | tf_op jit(solution)/shard_map/round/pallas_call | solution.py:494
  83.0 4.2 %tail.1 = (bf16[1024,2048]{1,0:T(8,128)(2,1)}, f32[256,1024]{1,0:T(8,128)}) custom-call(bf16[1024,256]{1,0:T(8,128)(2,1)} %get-tuple-element.9.hidt, bf16[256,2048]{1,0:T(8,128)(2,1)} %get-tuple-element.10.dn, bf16[1024,256]{1,0:T(8,128)(2,1)} %get-tuple-element.11.ag), custom_call_target="tpu_custom_call" | custom-call | tf_op jit(solution)/shard_map/tail/pallas_call | solution.py:563

commit v3 on v2

--- a/solution.py
+++ b/solution.py
@@ -74,28 +74,25 @@
     loads = [pltpu.make_async_copy(hidt, hv, sem.at[0])]
     loads += [pltpu.make_async_copy(dn.at[:, cols[i]], dv.at[:, cols[i]], sem.at[1 + i]) for i in range(4)]
     loads.append(pltpu.make_async_copy(ag, av, sem.at[5]))
-    for c in loads:
+    for c in loads[5:] + loads[:5]:
         c.start()
+    loads[5].wait()
+    iv[...] = jnp.transpose(av[...].astype(F32))
+    outs = [pltpu.make_async_copy(iv, ing_o, osem.at[4])]
+    outs[0].start()
     loads[0].wait()
-    outs = []
     for i in range(4):
         loads[1 + i].wait()
         gv[:, cols[i]] = jnp.dot(hv[...], dv[:, cols[i]], preferred_element_type=F32).astype(BF)
         outs.append(pltpu.make_async_copy(gv.at[:, cols[i]], hg_o.at[:, cols[i]], osem.at[i]))
         outs[-1].start()
-        if i == 2:
-            loads[5].wait()
-            iv[...] = jnp.transpose(av[...].astype(F32))
-            outs.append(pltpu.make_async_copy(iv, ing_o, osem.at[4]))
-            outs[-1].start()
     for c in outs:
         c.wait()
 
 
 FAR = (4, 3, 5, 2, 6, 1, 7, 0)
 FAR_X = (2, 1, 3, 0)
-BACK = (0, 1, 7, 4, 3, 5, 2, 6)
-SOON = (0, 1, 7, 2, 6, 3, 5, 4)
+NEAR = (0, 1, 7, 2, 6, 3, 5, 4)
 
 
 def kernel(
@@ -104,7 +101,7 @@
     ids, bias, tok, lab, table, inw, byte, outt,
     w, hid, fs, fr, sb, r2, ft, f, rx, la, lb, xf, bp, gp, gq, ga, gb, na, nb, ms, er, cm, cr, ta, tx, g_in,
     d_in, dn, hb, a1, a1s, a2, ag, hidt, chosen_s, like,
-    sl, sw, so, r1s, r1r, r2s, r2r, gs, gr, r3s, r3r, e1s, e1r, e2s, e2r, r4s, r4r, r5s, r5r, r6s, r6r,
+    on_x, on_z, sl, sw, so, r1s, r1r, r2s, r2r, gs, gr, r3s, r3r, e1s, e1r, e2s, e2r, r4s, r4r, r5s, r5r, r6s, r6r,
     p1s, p1r, p2s, p2r, p3s, p3r, p4s, p4r,
 ):
     rem, div = lax.rem, lax.div
@@ -149,23 +146,25 @@
         c.start()
 
     bar = pltpu.get_barrier_semaphore()
-    for dz in FAR:
-        for dx in FAR_X:
-            for dh in range(2):
-                for dk in range(2):
-                    if dx or dz or dh or dk:
-                        to = (xz16[dx][dz] + los[dh], his[dh] * 2 + ks[dk])
-                        pl.semaphore_signal(bar, inc=1, device_id=to, device_id_type=MESH)
-    for dx in range(4):
-        pl.semaphore_signal(bar, inc=1, device_id=(xz16[dx][0] + 1 - lo, grp), device_id_type=MESH)
+    along_x = [(xz16[dx][0] + lo, grp) for dx in (2, 1, 3)]
+    along_z = [(xz16[0][dz] + lo, grp) for dz in FAR[:7]]
+    beside = [
+        (xz16[0][0] + los[dl], his[dh] * 2 + ks[dk])
+        for dl in range(2) for dh in range(2) for dk in range(2) if dl or dh or dk
+    ]
+    for to in along_z + along_x + beside:
+        pl.semaphore_signal(bar, inc=1, device_id=to, device_id_type=MESH)
 
     m = iota((256, 256), 1)
     mhi, mx, mz, mp, mk = m % 2, (m // 2) % 4, (m // 8) % 8, (m // 64) % 2, m // 128
     owner = (mx * 16 + mz * 2 + (mp + mhi) % 2) * 4 + mhi * 2 + mk
     order = (iota((256, 256), 0) == owner).astype(BF)
     ins[0].wait()
-    picks = (iota((1024, 256), 0) == ids[...]).astype(F32).astype(BF)
-    picks = mm(picks, order, 1, 0)
+    upper = ids[...] // 32
+    halves = jnp.concatenate([upper, ids[...] - upper * 32], axis=0)
+    halves = mm(jnp.broadcast_to(halves[:, None], (2, 8, 256)).reshape(16, 256).astype(F32), order, 1, 0)
+    sorted_ids = (halves[0:1] * 32 + halves[8:9]).astype(jnp.int32)
+    picks = (iota((1024, 256), 0) == sorted_ids).astype(F32).astype(BF)
     ins[1].wait()
     chosen = mm(picks, table[...], 0, 0).astype(BF)
     chosen_s[...] = chosen
@@ -182,7 +181,9 @@
             2, 2, 8, 8, CW
         )
 
-    pl.semaphore_wait(bar, 131)
+    pl.semaphore_wait(bar, 17)
+    for to in along_x:
+        pl.semaphore_signal(on_x, inc=1, device_id=to, device_id_type=MESH)
 
     c1 = []
     for dz in FAR:
@@ -196,6 +197,9 @@
     gp[512:768, :] = mm(byte[...], byte[...], 1, 1)
     cg = remote(gp, gq, gs.at[0], gr.at[0], partner)
     cg.start()
+    pl.semaphore_wait(on_x, 3)
+    for to in along_z:
+        pl.semaphore_signal(on_z, inc=1, device_id=to, device_id_type=MESH)
     diag = iota((256, 256), 0) == iota((256, 256), 1)
     ra = pl.ds(pl.multiple_of(k * 160 + x * 40, 8), 40)
     rb = pl.ds(pl.multiple_of(k * 256 + x * 64, 64), 64)
@@ -240,6 +244,7 @@
     to_c = [hi_d * 2 + cores[q] for q in range(2)]
     mine = [to_c[q] == grp for q in range(2)]
     n_self = mine[0].astype(jnp.int32) + mine[1].astype(jnp.int32)
+    pl.semaphore_wait(on_z, 7)
     for i, dz in enumerate(FAR):
         drain(r2.at[:, zs[dz]], r2r.at[dz])
         both = r2[0, zs[dz]].astype(F32) + r2[1, zs[dz]].astype(F32)
@@ -365,31 +370,30 @@
         else:
             c.start()
 
-    z4 = [rem(z + d, 4) for d in (0, 1, 3, 2)]
     his_a = [rem(p + 1 - par, 2) for par in range(2)]
-    for step in range(8):
-        dz = BACK[step]
+    for dz in NEAR:
         for xh in range(2):
             for dk in range(2):
                 slot = 16 + xh * 8 + zs[dz]
                 to = (32 + xh * 16 + zs[dz] * 2 + 1 - hi, (1 - lo) * 2 + ks[dk])
                 give(slot, ks[dk], k, to, (8 - dz) % 8, dz == 0)
-        zr = z4[step // 2]
-        za = k * 4 + zr
-        back = rem(z - za + 8, 8)
-        par = step % 2
-        for q in range(2):
-            for dk in range(2):
-                slot = (zr * 2 + par) * 2 + q
-                to = (hi * 16 + za * 2 + 1 - par, his_a[par] * 2 + ks[dk])
-                give(slot, ks[dk], q, to, back, step // 2 == 0)
+
+        @pl.when(div(zs[dz], 4) == k)
+        def _(dz=dz):
+            for par in range(2):
+                for q in range(2):
+                    for dk in range(2):
+                        slot = (rem(zs[dz], 4) * 2 + par) * 2 + q
+                        to = (hi * 16 + zs[dz] * 2 + 1 - par, his_a[par] * 2 + ks[dk])
+                        give(slot, ks[dk], q, to, (8 - dz) % 8, dz == 0)
+
     for q in range(2):
 
         @pl.when(mine[q])
         def _(q=q):
             g_in[q, z, x] = tx[k, :, slots[q]]
 
-    for dz in SOON:
+    for dz in NEAR:
         if dz:
             drain(like.at[pl.ds(0, 8)], r4r.at[dz])
         else:
@@ -401,7 +405,7 @@
 
         for to in (n1, n2):
             remote(g_in.at[:, zs[dz]], d_in.at[k, p, :, zs[dz]], r5s, r5r.at[dz], to).start()
-    for dz in SOON:
+    for dz in NEAR:
         drain(d_in.at[k, :, :, zs[dz]], r5r.at[dz])
         region = d_in.at[k, :, :, zs[dz]]
         remote(region, region, r6s, r6r, partner).start()
@@ -541,6 +545,7 @@
             V((1024, 256), BF),
             V((256, 256), BF),
             V((64, 2, 8, 128), BF),
+            pltpu.SemaphoreType.REGULAR, pltpu.SemaphoreType.REGULAR,
             dma((8,)), dma((CH,)), dma((3,)),
             dma(()), dma((8,)),
             dma(()), dma((8,)),

time: 89 us -> 86.7 us (0.974)
  Pallas kernels: 86.5 us -> 84.2 us
    pallas_call x1, Pallas kernels: 82.4 us -> 80.1 us  [local(): pl.pallas_call(kernel, out_shape=(S((1024, 256), BF), S((256, 2048), BF),...]
where the time goes in v3:
time: 86.7 us; the launch traced here: 86.6 us
  Pallas kernels  84.2 us (97%)
  between operations  2.39 us (3%)
    pallas_call x1, Pallas kernels, local(): pl.pallas_call(kernel, out_shape=(S((1024, 256), BF), S((256, 2048), BF),...  80.1 us
    pallas_call x1, Pallas kernels, local(): pl.pallas_call(tail_kernel, out_shape=(S((1024, 2048), BF), S((256, 1024)...  4.06 us

profile of v3, /device:TPU:2, one launch (start us, length us, event | category | flops | bytes accessed | tf_op | source)
XLA Modules:
  0.0 86.6 jit_solution(758073654290678587)
XLA Ops:
  0.6 80.1 %round.1 = (bf16[1024,256]{1,0:T(8,128)(2,1)}, bf16[256,2048]{1,0:T(8,128)(2,1)}, bf16[1024,256]{1,0:T(8,128)(2,1)}, f32[1]{0:T(128)}) custom-call(s32[1,256]{1,0:T(1,128)} %bitcast.3, bf16[1024,256]{1,0:T(8,128)(2,1)} %table_h.1, bf16[256,1024]{1,0:T(8,128)(2,1)} %inw_h.1, f32[1,1024]{1,0:T(1,128)} %bitcast.2, bf16[1024,2048]{1,0:T(8,128)(2,1)} %w_hbm.1, ...), custom_call_target="tpu_custom_call" | custom-call | tf_op jit(solution)/shard_map/round/pallas_call | solution.py:498
  80.7 4.1 %tail.1 = (bf16[1024,2048]{1,0:T(8,128)(2,1)}, f32[256,1024]{1,0:T(8,128)}) custom-call(bf16[1024,256]{1,0:T(8,128)(2,1)} %get-tuple-element.9.hidt, bf16[256,2048]{1,0:T(8,128)(2,1)} %get-tuple-element.10.dn, bf16[1024,256]{1,0:T(8,128)(2,1)} %get-tuple-element.11.ag), custom_call_target="tpu_custom_call" | custom-call | tf_op jit(solution)/shard_map/tail/pallas_call | solution.py:568

commit v4 on v3

--- a/solution.py
+++ b/solution.py
@@ -74,18 +74,21 @@
     loads = [pltpu.make_async_copy(hidt, hv, sem.at[0])]
     loads += [pltpu.make_async_copy(dn.at[:, cols[i]], dv.at[:, cols[i]], sem.at[1 + i]) for i in range(4)]
     loads.append(pltpu.make_async_copy(ag, av, sem.at[5]))
-    for c in loads[5:] + loads[:5]:
+    for c in loads:
         c.start()
-    loads[5].wait()
-    iv[...] = jnp.transpose(av[...].astype(F32))
-    outs = [pltpu.make_async_copy(iv, ing_o, osem.at[4])]
-    outs[0].start()
     loads[0].wait()
+    outs = []
     for i in range(4):
         loads[1 + i].wait()
+        if i == 1:
+            loads[5].wait()
+            iv[...] = jnp.transpose(av[...].astype(F32))
         gv[:, cols[i]] = jnp.dot(hv[...], dv[:, cols[i]], preferred_element_type=F32).astype(BF)
         outs.append(pltpu.make_async_copy(gv.at[:, cols[i]], hg_o.at[:, cols[i]], osem.at[i]))
         outs[-1].start()
+        if i == 1:
+            outs.append(pltpu.make_async_copy(iv, ing_o, osem.at[4]))
+            outs[-1].start()
     for c in outs:
         c.wait()
 
@@ -99,7 +102,7 @@
     ids_h, table_h, inw_h, bias_h, w_hbm, tok_h, lab_h, byte_h, outt_h,
     ag_o, dn_o, hidt_o, loss_o,
     ids, bias, tok, lab, table, inw, byte, outt,
-    w, hid, fs, fr, sb, r2, ft, f, rx, la, lb, xf, bp, gp, gq, ga, gb, na, nb, ms, er, cm, cr, ta, tx, g_in,
+    w, hid, fs, fr, sb, r2, ft, f, rx, la, lb, xf, bp, gp, gq, ga, gb, na, nb, gd, nd, ms, er, cm, cr, ta, tx, g_in,
     d_in, dn, hb, a1, a1s, a2, ag, hidt, chosen_s, like,
     on_x, on_z, sl, sw, so, r1s, r1r, r2s, r2r, gs, gr, r3s, r3r, e1s, e1r, e2s, e2r, r4s, r4r, r5s, r5r, r6s, r6r,
     p1s, p1r, p2s, p2r, p3s, p3r, p4s, p4r,
@@ -128,6 +131,7 @@
     partner = (head, hi * 2 + 1 - k)
     n1 = (xz16[0][0] + 1 - lo, grp)
     n2 = (xz16[0][0] + 1 - lo, (1 - hi) * 2 + k)
+    across = (head, (1 - hi) * 2 + k)
 
     ins = [
         pltpu.make_async_copy(src, dst, sl.at[i])
@@ -200,24 +204,33 @@
     pl.semaphore_wait(on_x, 3)
     for to in along_z:
         pl.semaphore_signal(on_z, inc=1, device_id=to, device_id_type=MESH)
+    is_a = x < 2
+    stays = jnp.logical_not(is_a) & (hi == lo)
+    parts = jnp.logical_not(is_a) & (hi != lo)
+    moves = jnp.logical_not(stays)
+    lo_b = jnp.where(is_a, 1 - lo, hi)
     diag = iota((256, 256), 0) == iota((256, 256), 1)
-    ra = pl.ds(pl.multiple_of(k * 160 + x * 40, 8), 40)
+    ra = pl.ds(pl.multiple_of(k * 128 + x * 32, 32), 32)
     rb = pl.ds(pl.multiple_of(k * 256 + x * 64, 64), 64)
     cg2 = [
         remote(ga.at[ra], na.at[ra], gs.at[1], gr.at[1], n2),
         remote(gb.at[rb], nb.at[rb], gs.at[2], gr.at[2], n2),
+        remote(gd, nd, gs.at[3], gr.at[7], n2),
     ]
     for i, dz in enumerate(FAR):
         c1[i].wait_recv()
         sb[:, zs[dz]] = (fs[k, :, zs[dz]] + fr[:, zs[dz]]).astype(BF)
-        remote(sb.at[1 - p, zs[dz]], r2.at[0, zs[dz]], r2s, r2r.at[dz], n1).start()
-        remote(sb.at[p, zs[dz]], r2.at[1, zs[dz]], r2s, r2r.at[dz], n2).start()
+        half = sb.at[1 - p, zs[dz]]
+        pl.when(parts)(remote(half, r2.at[1, zs[dz]], r2s, r2r.at[1, dz], across).start)
+        pl.when(jnp.logical_not(parts))(remote(half, r2.at[0, zs[dz]], r2s, r2r.at[0, dz], n1).start)
+        pl.when(is_a)(remote(sb.at[p, zs[dz]], r2.at[1, zs[dz]], r2s, r2r.at[1, dz], n2).start)
+        pl.when(parts)(remote(sb.at[p, zs[dz]], r2.at[2, zs[dz]], r2s, r2r.at[2, dz], n2).start)
         if i == 5:
             cg.wait_recv()
             gsum = gp[...] + gq[...]
-            ga[0:256, :] = gsum[0:256]
-            ga[256:320, :] = jnp.broadcast_to(
-                jnp.sum(jnp.where(diag, gsum[512:768], 0.0), 0, keepdims=True), (64, 256)
+            ga[...] = gsum[0:256]
+            gd[...] = jnp.broadcast_to(
+                jnp.sum(jnp.where(diag, gsum[512:768], 0.0), 0, keepdims=True), (8, 256)
             )
             gb[...] = gsum[256:768].astype(BF)
             for c in cg2:
@@ -236,9 +249,8 @@
     co = [pltpu.make_async_copy(hidt, hidt_o, so.at[0])]
     co[0].start()
 
-    is_a = x < 2
-    slots = [jnp.where(is_a, (rem(z, 4) * 2 + 1 - lo) * 2 + q, 16 + 8 * (x - 2) + z) for q in range(2)]
-    hi_d = jnp.where(is_a, x, 1 - lo)
+    slots = [jnp.where(is_a, (rem(z, 4) * 2 + lo_b) * 2 + q, 16 + 8 * (x - 2) + z) for q in range(2)]
+    hi_d = jnp.where(is_a, x, hi)
     lo_d = rem(p + hi_d, 2)
     cores = [jnp.where(is_a, div(z, 4), q) for q in range(2)]
     to_c = [hi_d * 2 + cores[q] for q in range(2)]
@@ -246,8 +258,12 @@
     n_self = mine[0].astype(jnp.int32) + mine[1].astype(jnp.int32)
     pl.semaphore_wait(on_z, 7)
     for i, dz in enumerate(FAR):
-        drain(r2.at[:, zs[dz]], r2r.at[dz])
-        both = r2[0, zs[dz]].astype(F32) + r2[1, zs[dz]].astype(F32)
+        first = r2.at[0, zs[dz]]
+        pl.when(moves)(pltpu.make_async_copy(first, first, r2r.at[0, dz]).wait)
+        pl.when(jnp.logical_not(parts))(pltpu.make_async_copy(first, first, r2r.at[1, dz]).wait)
+        pl.when(parts)(pltpu.make_async_copy(first, first, r2r.at[2, dz]).wait)
+        second = jnp.where(parts, r2[2, zs[dz]], r2[1, zs[dz]])
+        both = jnp.where(stays, sb[p, zs[dz]], r2[0, zs[dz]]).astype(F32) + second.astype(F32)
         for q in range(2):
             for j in range(8):
                 at = (q * 8 + j) * 128
@@ -262,13 +278,12 @@
                     c.start()
                 else:
                     pl.when(jnp.logical_not(mine[q]))(c.start)
-        if i == 6:
-            for c in cg2:
-                c.wait_recv()
-            for dx in (2, 1, 3):
-                to = (xz16[dx][0] + lo, grp)
-                remote(na.at[ra], na.at[ra], gs.at[1], gr.at[3], to).start()
-                remote(nb.at[rb], nb.at[rb], gs.at[2], gr.at[4], to).start()
+    for c in cg2:
+        c.wait_recv()
+    for dx in (2, 1, 3):
+        to = (xz16[dx][0] + lo, grp)
+        remote(na.at[ra], na.at[ra], gs.at[1], gr.at[3], to).start()
+        remote(nb.at[rb], nb.at[rb], gs.at[2], gr.at[4], to).start()
     for q in range(2):
 
         @pl.when(mine[q])
@@ -285,16 +300,6 @@
 
     wait_all(r3r)
 
-    drain(na.at[pl.ds(0, 120)], gr.at[3])
-    drain(nb.at[pl.ds(0, 192)], gr.at[4])
-    ha = pl.ds(pl.multiple_of(k * 160, 8), 160)
-    hbb = pl.ds(pl.multiple_of(k * 256, 256), 256)
-    cg3 = [
-        remote(na.at[ha], na.at[ha], gs.at[1], gr.at[5], partner),
-        remote(nb.at[hbb], nb.at[hbb], gs.at[2], gr.at[6], partner),
-    ]
-    for c in cg3:
-        c.start()
     for c in range(4):
         at = jnp.transpose(rx[c // 2, c % 2, 0:16].astype(F32).reshape(128, 128))
         for d8 in range(8):
@@ -321,10 +326,20 @@
     for o in range(1, 4):
         c_, to = members[o]
         remote(ms.at[c_], er.at[o], e1s, e1r, to).start()
+    drain(na.at[pl.ds(0, 96)], gr.at[3])
+    drain(nb.at[pl.ds(0, 192)], gr.at[4])
+    ha = pl.ds(pl.multiple_of(k * 128, 128), 128)
+    hbb = pl.ds(pl.multiple_of(k * 256, 256), 256)
+    cg3 = [
+        remote(na.at[ha], na.at[ha], gs.at[1], gr.at[5], partner),
+        remote(nb.at[hbb], nb.at[hbb], gs.at[2], gr.at[6], partner),
+    ]
+    for c in cg3:
+        c.start()
     for c in cg3:
         c.wait_recv()
-    obt = ga[0:256, :] + na[0:256, :]
-    bb = ga[256:257, :] + na[256:257, :]
+    obt = ga[...] + na[...]
+    bb = gd[0:1, :] + nd[0:1, :]
     grams = gb[...].astype(F32) + nb[...].astype(F32)
     oo, bbm = grams[0:256].astype(BF), grams[256:512].astype(BF)
     scale = lax.rsqrt(bb * (1 / 4096) + EPS)
@@ -375,7 +390,7 @@
         for xh in range(2):
             for dk in range(2):
                 slot = 16 + xh * 8 + zs[dz]
-                to = (32 + xh * 16 + zs[dz] * 2 + 1 - hi, (1 - lo) * 2 + ks[dk])
+                to = (32 + xh * 16 + zs[dz] * 2 + lo, hi * 2 + ks[dk])
                 give(slot, ks[dk], k, to, (8 - dz) % 8, dz == 0)
 
         @pl.when(div(zs[dz], 4) == k)
@@ -403,11 +418,21 @@
                 def _(n=n):
                     drain(like.at[pl.ds(0, 8 - n)], r4r.at[0])
 
-        for to in (n1, n2):
-            remote(g_in.at[:, zs[dz]], d_in.at[k, p, :, zs[dz]], r5s, r5r.at[dz], to).start()
+        part, spot = g_in.at[:, zs[dz]], d_in.at[k, p, :, zs[dz]]
+        pl.when(moves)(remote(part, spot, r5s, r5r.at[0, dz], n1).start)
+        pl.when(moves)(remote(part, spot, r5s, r5r.at[1, dz], n2).start)
+        pl.when(stays)(remote(part, spot, r5s, r5r.at[2, dz], across).start)
+
+    @pl.when(stays)
+    def _():
+        d_in[k, p] = g_in[...]
+
     for dz in NEAR:
-        drain(d_in.at[k, :, :, zs[dz]], r5r.at[dz])
         region = d_in.at[k, :, :, zs[dz]]
+        one = d_in.at[k, 0, :, zs[dz]]
+        pl.when(jnp.logical_not(parts))(pltpu.make_async_copy(one, one, r5r.at[0, dz]).wait)
+        pl.when(moves)(pltpu.make_async_copy(one, one, r5r.at[1, dz]).wait)
+        pl.when(parts)(pltpu.make_async_copy(one, one, r5r.at[2, dz]).wait)
         remote(region, region, r6s, r6r, partner).start()
     drain(d_in.at[1 - k], r6r)
     for kp in range(4):
@@ -472,13 +497,16 @@
     co[2].start()
 
     drain(fr, r1s)
-    drain(r2, r2s)
+    pl.when(stays)(pltpu.make_async_copy(r2.at[0], r2.at[0], r2s).wait)
+    pl.when(moves)(pltpu.make_async_copy(r2.at[pl.ds(0, 2)], r2.at[pl.ds(0, 2)], r2s).wait)
     drain(gq, gs.at[0])
     drain(na, gs.at[1])
     drain(nb, gs.at[2])
+    drain(nd, gs.at[3])
     drain(er.at[pl.ds(1, 3)], e1s)
     drain(er.at[pl.ds(1, 3)], e2s)
-    drain(d_in.at[0], r5s)
+    pl.when(stays)(pltpu.make_async_copy(g_in, g_in, r5s).wait)
+    pl.when(moves)(pltpu.make_async_copy(d_in.at[0], d_in.at[0], r5s).wait)
     drain(d_in.at[0], r6s)
     drain(a1.at[pl.ds(1, 7)], p1s)
     drain(a2.at[pl.ds(1, 7)], p2s)
@@ -514,7 +542,7 @@
             V((2, 2, 8, 8, 2048), F32),
             V((2, 8, 8, 2048), F32),
             V((2, 8, 8, 2048), BF),
-            V((2, 8, 8, 2048), BF),
+            V((3, 8, 8, 2048), BF),
             V((2, 512, 128), F32),
             V((2, 8, 4, 2, 8, 128), BF),
             V((2, 2, 32, 8, 128), BF),
@@ -524,10 +552,12 @@
             V((256, 1024), BF),
             V((768, 256), F32),
             V((768, 256), F32),
-            V((320, 256), F32),
+            V((256, 256), F32),
             V((512, 256), BF),
-            V((320, 256), F32),
+            V((256, 256), F32),
             V((512, 256), BF),
+            V((8, 256), F32),
+            V((8, 256), F32),
             V((4, 64, 256), BF),
             V((4, 64, 256), BF),
             V((64, 256), BF),
@@ -548,12 +578,12 @@
             pltpu.SemaphoreType.REGULAR, pltpu.SemaphoreType.REGULAR,
             dma((8,)), dma((CH,)), dma((3,)),
             dma(()), dma((8,)),
-            dma(()), dma((8,)),
-            dma((3,)), dma((7,)),
+            dma(()), dma((3, 8)),
+            dma((4,)), dma((8,)),
             dma(()), dma(()),
             dma(()), dma(()), dma(()), dma(()),
             dma(()), dma((8,)),
-            dma(()), dma((8,)), dma(()), dma(()),
+            dma(()), dma((3, 8)), dma(()), dma(()),
             dma(()), dma((2,)), dma(()), dma(()),
             dma(()), dma((8,)), dma(()), dma(()),
         ],

time: 86.7 us -> 84.9 us (0.979)
  Pallas kernels: 84.2 us -> 82.4 us
    pallas_call x1, Pallas kernels: 80.1 us -> 78.3 us  [local(): pl.pallas_call(kernel, out_shape=(S((1024, 256), BF), S((256, 2048), BF),...]
where the time goes in v4:
time: 84.9 us; the launch traced here: 84.8 us
  Pallas kernels  82.4 us (97%)
  between operations  2.39 us (3%)
    pallas_call x1, Pallas kernels, local(): pl.pallas_call(kernel, out_shape=(S((1024, 256), BF), S((256, 2048), BF),...  78.3 us
    pallas_call x1, Pallas kernels, local(): pl.pallas_call(tail_kernel, out_shape=(S((1024, 2048), BF), S((256, 1024)...  4.09 us

profile of v4, /device:TPU:2, one launch (start us, length us, event | category | flops | bytes accessed | tf_op | source)
XLA Modules:
  0.0 84.8 jit_solution(17684329843933461788)
XLA Ops:
  0.6 78.3 %round.1 = (bf16[1024,256]{1,0:T(8,128)(2,1)}, bf16[256,2048]{1,0:T(8,128)(2,1)}, bf16[1024,256]{1,0:T(8,128)(2,1)}, f32[1]{0:T(128)}) custom-call(s32[1,256]{1,0:T(1,128)} %bitcast.3, bf16[1024,256]{1,0:T(8,128)(2,1)} %table_h.1, bf16[256,1024]{1,0:T(8,128)(2,1)} %inw_h.1, f32[1,1024]{1,0:T(1,128)} %bitcast.2, bf16[1024,2048]{1,0:T(8,128)(2,1)} %w_hbm.1, ...), custom_call_target="tpu_custom_call" | custom-call | tf_op jit(solution)/shard_map/round/pallas_call | solution.py:526
  79.0 4.1 %tail.1 = (bf16[1024,2048]{1,0:T(8,128)(2,1)}, f32[256,1024]{1,0:T(8,128)}) custom-call(bf16[1024,256]{1,0:T(8,128)(2,1)} %get-tuple-element.9.hidt, bf16[256,2048]{1,0:T(8,128)(2,1)} %get-tuple-element.10.dn, bf16[1024,256]{1,0:T(8,128)(2,1)} %get-tuple-element.11.ag), custom_call_target="tpu_custom_call" | custom-call | tf_op jit(solution)/shard_map/tail/pallas_call | solution.py:598

commit v5 on v4

--- a/solution.py
+++ b/solution.py
@@ -434,38 +434,42 @@
         pl.when(moves)(pltpu.make_async_copy(one, one, r5r.at[1, dz]).wait)
         pl.when(parts)(pltpu.make_async_copy(one, one, r5r.at[2, dz]).wait)
         remote(region, region, r6s, r6r, partner).start()
-    drain(d_in.at[1 - k], r6r)
-    for kp in range(4):
-        xd = d_in[kp // 2, kp % 2].astype(F32).reshape(1024, 128)
-        ft[0] = xd[0:512]
-        ft[1] = xd[512:1024]
-        for j in range(16):
-            dn[kp * 64 : (kp + 1) * 64, j * 128 : (j + 1) * 128] = ft[
-                j // 8, pl.ds(j % 8, 64, stride=8), :
-            ].astype(BF)
+    turn = [rem(zn - z + 14, 8) * 16 for zn in range(8)]
+    peers = [(xs[o // 2], los[o % 2], (xz16[o // 2][0] + los[o % 2], grp)) for o in range(8)]
+    for half in range(2):
+        if half:
+            drain(d_in.at[1 - k], r6r)
+        row = pl.multiple_of(ks[half] * 128, 128)
+        for p_ in range(2):
+            xd = d_in[ks[half], p_].astype(F32).reshape(1024, 128)
+            ft[0] = xd[0:512]
+            ft[1] = xd[512:1024]
+            for j in range(16):
+                dn[pl.ds(row + p_ * 64, 64), j * 128 : (j + 1) * 128] = ft[
+                    j // 8, pl.ds(j % 8, 64, stride=8), :
+                ].astype(BF)
+        for i in range(4):
+            part = mm(w[i * 256 : (i + 1) * 256, :], dn[pl.ds(row, 128), :], 1, 1).astype(BF)
+            for l_ in range(2):
+                for zn in range(8):
+                    at = l_ * 128 + zn * 16
+                    hb[half, i, l_, pl.ds(pl.multiple_of(turn[zn], 16), 16), :] = part[at : at + 16]
+        for h in range(2):
+            rows = pl.ds(h * 64, 64)
+            for o in (4, 5, 2, 3, 6, 7, 1):
+                x_, lo_, to = peers[o]
+                src = hb.at[half, x_, lo_, rows]
+                remote(src, a1.at[half, o, rows], p1s, p1r.at[half, h], to).start()
     co.append(pltpu.make_async_copy(dn, dn_o, so.at[1]))
     co[1].start()
-
-    turn = [rem(zn - z + 14, 8) * 16 for zn in range(8)]
-    for i in range(4):
-        part = mm(w[i * 256 : (i + 1) * 256, :], dn[...], 1, 1).astype(BF)
-        for l_ in range(2):
-            for zn in range(8):
-                at = l_ * 128 + zn * 16
-                hb[i, l_, pl.ds(pl.multiple_of(turn[zn], 16), 16), :] = part[at : at + 16]
-    peers = [(xs[o // 2], los[o % 2], (xz16[o // 2][0] + los[o % 2], grp)) for o in range(8)]
     for h in range(2):
         rows = pl.ds(h * 64, 64)
-        for o in (4, 5, 2, 3, 6, 7, 1):
-            x_, lo_, to = peers[o]
-            remote(hb.at[x_, lo_, rows], a1.at[o, rows], p1s, p1r.at[h], to).start()
-    for h in range(2):
-        rows = pl.ds(h * 64, 64)
-        acc = hb[x, lo, rows, :].astype(F32)
-        drain(a1.at[pl.ds(1, 7), rows], p1r.at[h])
-        for o in range(1, 8):
-            acc = acc + a1[o, rows, :].astype(F32)
-        a1s[rows, :] = acc.astype(BF)
+        for half in range(2):
+            acc = hb[half, x, lo, rows, :].astype(F32)
+            drain(a1.at[half, pl.ds(1, 7), rows], p1r.at[half, h])
+            for o in range(1, 8):
+                acc = acc + a1[half, o, rows, :].astype(F32)
+            a1s[rows, pl.ds(pl.multiple_of(ks[half] * 128, 128), 128)] = acc.astype(BF)
         for t in ((2, 1, 3, 0), (4, 7, 5, 6))[h]:
             dz = (t + 2) % 8
             if dz:
@@ -492,7 +496,7 @@
         rows = ag.at[pl.ds(pl.multiple_of(base + zs[(8 - dz) % 8] * 16, 16), 16)]
         for o in (4, 5, 2, 3, 6, 7, 1):
             remote(rows, rows, p4s, p4r, peers[o][2]).start()
-    drain(a1.at[pl.ds(1, 7)], p4r)
+    drain(a1.at[:, pl.ds(1, 7)], p4r)
     co.append(pltpu.make_async_copy(ag, ag_o, so.at[2]))
     co[2].start()
 
@@ -508,10 +512,10 @@
     pl.when(stays)(pltpu.make_async_copy(g_in, g_in, r5s).wait)
     pl.when(moves)(pltpu.make_async_copy(d_in.at[0], d_in.at[0], r5s).wait)
     drain(d_in.at[0], r6s)
-    drain(a1.at[pl.ds(1, 7)], p1s)
+    drain(a1.at[:, pl.ds(1, 7)], p1s)
     drain(a2.at[pl.ds(1, 7)], p2s)
     drain(a2.at[pl.ds(1, 7)], p3s)
-    drain(a1.at[pl.ds(1, 7)], p4s)
+    drain(a1.at[:, pl.ds(1, 7)], p4s)
     wait_all(r3s)
     wait_all(r4s)
     for c in co:
@@ -567,8 +571,8 @@
             V((2, 8, 4, 2, 8, 128), BF),
             V((2, 2, 2, 8, 4, 2, 8, 128), BF),
             V((256, 2048), BF),
-            V((4, 2, 128, 256), BF),
-            V((8, 128, 256), BF),
+            V((2, 4, 2, 128, 128), BF),
+            V((2, 8, 128, 128), BF),
             V((128, 256), BF),
             V((8, 16, 256), BF),
             V((1024, 256), BF),
@@ -584,7 +588,7 @@
             dma(()), dma(()), dma(()), dma(()),
             dma(()), dma((8,)),
             dma(()), dma((3, 8)), dma(()), dma(()),
-            dma(()), dma((2,)), dma(()), dma(()),
+            dma(()), dma((2, 2)), dma(()), dma(()),
             dma(()), dma((8,)), dma(()), dma(()),
         ],
         compiler_params=pltpu.CompilerParams(

time: 84.9 us -> 83.8 us (0.987); the launches traced: 84.8 us -> 82.6 us
  Pallas kernels: 82.4 us -> 80.2 us
    pallas_call x1, Pallas kernels: 78.3 us -> 76.2 us  [local(): pl.pallas_call(kernel, out_shape=(S((1024, 256), BF), S((256, 2048), BF),...]
where the time goes in v5:
time: 83.8 us; the launch traced here: 82.6 us
  Pallas kernels  80.2 us (96%)
  between operations  2.39 us (3%)
    pallas_call x1, Pallas kernels, local(): pl.pallas_call(kernel, out_shape=(S((1024, 256), BF), S((256, 2048), BF),...  76.2 us
    pallas_call x1, Pallas kernels, local(): pl.pallas_call(tail_kernel, out_shape=(S((1024, 2048), BF), S((256, 1024)...  4.08 us

profile of v5, /device:TPU:2, one launch (start us, length us, event | category | flops | bytes accessed | tf_op | source)
XLA Modules:
  0.0 82.6 jit_solution(1365392690673650535)
XLA Ops:
  0.6 76.2 %round.1 = (bf16[1024,256]{1,0:T(8,128)(2,1)}, bf16[256,2048]{1,0:T(8,128)(2,1)}, bf16[1024,256]{1,0:T(8,128)(2,1)}, f32[1]{0:T(128)}) custom-call(s32[1,256]{1,0:T(1,128)} %bitcast.3, bf16[1024,256]{1,0:T(8,128)(2,1)} %table_h.1, bf16[256,1024]{1,0:T(8,128)(2,1)} %inw_h.1, f32[1,1024]{1,0:T(1,128)} %bitcast.2, bf16[1024,2048]{1,0:T(8,128)(2,1)} %w_hbm.1, ...), custom_call_target="tpu_custom_call" | custom-call | tf_op jit(solution)/shard_map/round/pallas_call | solution.py:530
  76.8 4.1 %tail.1 = (bf16[1024,2048]{1,0:T(8,128)(2,1)}, f32[256,1024]{1,0:T(8,128)}) custom-call(bf16[1024,256]{1,0:T(8,128)(2,1)} %get-tuple-element.9.hidt, bf16[256,2048]{1,0:T(8,128)(2,1)} %get-tuple-element.10.dn, bf16[1024,256]{1,0:T(8,128)(2,1)} %get-tuple-element.11.ag), custom_call_target="tpu_custom_call" | custom-call | tf_op jit(solution)/shard_map/tail/pallas_call | solution.py:602

commit v6 on v5

--- a/solution.py
+++ b/solution.py
@@ -178,29 +178,22 @@
     hidden = jnp.maximum(pre, 0.0)
     hid[...] = hidden.astype(BF)
 
-    for i in range(CH):
-        cols = pl.ds(i * CW, CW)
-        wc[i].wait()
-        fs[:, :, :, :, cols] = jnp.dot(hid[...], w[:, cols], preferred_element_type=F32).reshape(
-            2, 2, 8, 8, CW
-        )
-
-    pl.semaphore_wait(bar, 17)
-    for to in along_x:
-        pl.semaphore_signal(on_x, inc=1, device_id=to, device_id_type=MESH)
-
-    c1 = []
-    for dz in FAR:
-        c = remote(fs.at[1 - k, :, zs[dz]], fr.at[:, zs[dz]], r1s, r1r.at[dz], partner)
-        c.start()
-        c1.append(c)
-    ins[4].wait()
-    ins[5].wait()
-    gp[0:256, :] = mm(outt[...], byte[...], 1, 1)
-    gp[256:512, :] = mm(outt[...], outt[...], 1, 1)
-    gp[512:768, :] = mm(byte[...], byte[...], 1, 1)
-    cg = remote(gp, gq, gs.at[0], gr.at[0], partner)
-    cg.start()
+    qcols = [pl.ds(q * 1024, 1024) for q in range(2)]
+    for q in range(2):
+        for i in range(q * CH // 2, (q + 1) * CH // 2):
+            cols = pl.ds(i * CW, CW)
+            wc[i].wait()
+            fs[:, :, :, :, cols] = jnp.dot(hid[...], w[:, cols], preferred_element_type=F32).reshape(
+                2, 2, 8, 8, CW
+            )
+        if q == 0:
+            pl.semaphore_wait(bar, 17)
+            for to in along_x:
+                pl.semaphore_signal(on_x, inc=1, device_id=to, device_id_type=MESH)
+        for dz in FAR:
+            remote(
+                fs.at[1 - k, :, zs[dz], :, qcols[q]], fr.at[:, zs[dz], :, qcols[q]], r1s, r1r.at[q, dz], partner
+            ).start()
     pl.semaphore_wait(on_x, 3)
     for to in along_z:
         pl.semaphore_signal(on_z, inc=1, device_id=to, device_id_type=MESH)
@@ -217,24 +210,31 @@
         remote(gb.at[rb], nb.at[rb], gs.at[2], gr.at[2], n2),
         remote(gd, nd, gs.at[3], gr.at[7], n2),
     ]
-    for i, dz in enumerate(FAR):
-        c1[i].wait_recv()
-        sb[:, zs[dz]] = (fs[k, :, zs[dz]] + fr[:, zs[dz]]).astype(BF)
-        half = sb.at[1 - p, zs[dz]]
-        pl.when(parts)(remote(half, r2.at[1, zs[dz]], r2s, r2r.at[1, dz], across).start)
-        pl.when(jnp.logical_not(parts))(remote(half, r2.at[0, zs[dz]], r2s, r2r.at[0, dz], n1).start)
-        pl.when(is_a)(remote(sb.at[p, zs[dz]], r2.at[1, zs[dz]], r2s, r2r.at[1, dz], n2).start)
-        pl.when(parts)(remote(sb.at[p, zs[dz]], r2.at[2, zs[dz]], r2s, r2r.at[2, dz], n2).start)
-        if i == 5:
-            cg.wait_recv()
-            gsum = gp[...] + gq[...]
-            ga[...] = gsum[0:256]
-            gd[...] = jnp.broadcast_to(
-                jnp.sum(jnp.where(diag, gsum[512:768], 0.0), 0, keepdims=True), (8, 256)
-            )
-            gb[...] = gsum[256:768].astype(BF)
-            for c in cg2:
-                c.start()
+    for i in range(16):
+        q, dz = i // 8, FAR[i % 8]
+        got = fr.at[:, zs[dz], :, qcols[q]]
+        drain(got, r1r.at[q, dz])
+        sb[:, zs[dz], :, qcols[q]] = (fs[k, :, zs[dz], :, qcols[q]] + fr[:, zs[dz], :, qcols[q]]).astype(BF)
+        half, own = sb.at[1 - p, zs[dz], :, qcols[q]], sb.at[p, zs[dz], :, qcols[q]]
+        to_0, to_1 = r2.at[0, zs[dz], :, qcols[q]], r2.at[1, zs[dz], :, qcols[q]]
+        pl.when(parts)(remote(half, to_1, r2s, r2r.at[q, 1, dz], across).start)
+        pl.when(jnp.logical_not(parts))(remote(half, to_0, r2s, r2r.at[q, 0, dz], n1).start)
+        pl.when(moves)(remote(own, to_1, r2s, r2r.at[q, 1, dz], n2).start)
+        if i == 7:
+            ins[4].wait()
+            ins[5].wait()
+            gp[0:256, :] = mm(outt[...], byte[...], 1, 1)
+            gp[256:512, :] = mm(outt[...], outt[...], 1, 1)
+            gp[512:768, :] = mm(byte[...], byte[...], 1, 1)
+            cg = remote(gp, gq, gs.at[0], gr.at[0], partner)
+            cg.start()
+    cg.wait_recv()
+    gsum = gp[...] + gq[...]
+    ga[...] = gsum[0:256]
+    gd[...] = jnp.broadcast_to(jnp.sum(jnp.where(diag, gsum[512:768], 0.0), 0, keepdims=True), (8, 256))
+    gb[...] = gsum[256:768].astype(BF)
+    for c in cg2:
+        c.start()
 
     for d8 in range(8):
         perm = (iota((1024, 128), 0) == 8 * iota((1024, 128), 1) + d8).astype(F32)
@@ -257,27 +257,24 @@
     mine = [to_c[q] == grp for q in range(2)]
     n_self = mine[0].astype(jnp.int32) + mine[1].astype(jnp.int32)
     pl.semaphore_wait(on_z, 7)
-    for i, dz in enumerate(FAR):
-        first = r2.at[0, zs[dz]]
-        pl.when(moves)(pltpu.make_async_copy(first, first, r2r.at[0, dz]).wait)
-        pl.when(jnp.logical_not(parts))(pltpu.make_async_copy(first, first, r2r.at[1, dz]).wait)
-        pl.when(parts)(pltpu.make_async_copy(first, first, r2r.at[2, dz]).wait)
-        second = jnp.where(parts, r2[2, zs[dz]], r2[1, zs[dz]])
-        both = jnp.where(stays, sb[p, zs[dz]], r2[0, zs[dz]]).astype(F32) + second.astype(F32)
-        for q in range(2):
-            for j in range(8):
-                at = (q * 8 + j) * 128
-                ft[q, pl.ds(j, 8, stride=8), :] = both[:, at : at + 128]
-            f[q, zs[dz]] = ft[q, 0:64].astype(BF).reshape(4, 2, 8, 128)
+    for i in range(16):
+        q, dz = i // 8, FAR[i % 8]
+        first = r2.at[0, zs[dz], :, qcols[q]]
+        pl.when(moves)(pltpu.make_async_copy(first, first, r2r.at[q, 0, dz]).wait)
+        drain(first, r2r.at[q, 1, dz])
+        both = jnp.where(stays, sb[p, zs[dz], :, qcols[q]], r2[0, zs[dz], :, qcols[q]]).astype(F32)
+        both = both + r2[1, zs[dz], :, qcols[q]].astype(F32)
+        for j in range(8):
+            ft[q, pl.ds(j, 8, stride=8), :] = both[:, j * 128 : (j + 1) * 128]
+        f[q, zs[dz]] = ft[q, 0:64].astype(BF).reshape(4, 2, 8, 128)
         for dx in FAR_X:
-            for q in range(2):
-                c = remote(
-                    f.at[q, zs[dz], xs[dx]], rx.at[k, :, slots[q]], r3s, r3r, (xz16[dx][dz] + lo_d, to_c[q])
-                )
-                if dz or dx:
-                    c.start()
-                else:
-                    pl.when(jnp.logical_not(mine[q]))(c.start)
+            c = remote(
+                f.at[q, zs[dz], xs[dx]], rx.at[k, :, slots[q]], r3s, r3r, (xz16[dx][dz] + lo_d, to_c[q])
+            )
+            if dz or dx:
+                c.start()
+            else:
+                pl.when(jnp.logical_not(mine[q]))(c.start)
     for c in cg2:
         c.wait_recv()
     for dx in (2, 1, 3):
@@ -421,7 +418,7 @@
         part, spot = g_in.at[:, zs[dz]], d_in.at[k, p, :, zs[dz]]
         pl.when(moves)(remote(part, spot, r5s, r5r.at[0, dz], n1).start)
         pl.when(moves)(remote(part, spot, r5s, r5r.at[1, dz], n2).start)
-        pl.when(stays)(remote(part, spot, r5s, r5r.at[2, dz], across).start)
+        pl.when(stays)(remote(part, spot, r5s, r5r.at[0, dz], across).start)
 
     @pl.when(stays)
     def _():
@@ -430,9 +427,8 @@
     for dz in NEAR:
         region = d_in.at[k, :, :, zs[dz]]
         one = d_in.at[k, 0, :, zs[dz]]
-        pl.when(jnp.logical_not(parts))(pltpu.make_async_copy(one, one, r5r.at[0, dz]).wait)
+        drain(one, r5r.at[0, dz])
         pl.when(moves)(pltpu.make_async_copy(one, one, r5r.at[1, dz]).wait)
-        pl.when(parts)(pltpu.make_async_copy(one, one, r5r.at[2, dz]).wait)
         remote(region, region, r6s, r6r, partner).start()
     turn = [rem(zn - z + 14, 8) * 16 for zn in range(8)]
     peers = [(xs[o // 2], los[o % 2], (xz16[o // 2][0] + los[o % 2], grp)) for o in range(8)]
@@ -502,7 +498,7 @@
 
     drain(fr, r1s)
     pl.when(stays)(pltpu.make_async_copy(r2.at[0], r2.at[0], r2s).wait)
-    pl.when(moves)(pltpu.make_async_copy(r2.at[pl.ds(0, 2)], r2.at[pl.ds(0, 2)], r2s).wait)
+    pl.when(moves)(pltpu.make_async_copy(r2, r2, r2s).wait)
     drain(gq, gs.at[0])
     drain(na, gs.at[1])
     drain(nb, gs.at[2])
@@ -546,7 +542,7 @@
             V((2, 2, 8, 8, 2048), F32),
             V((2, 8, 8, 2048), F32),
             V((2, 8, 8, 2048), BF),
-            V((3, 8, 8, 2048), BF),
+            V((2, 8, 8, 2048), BF),
             V((2, 512, 128), F32),
             V((2, 8, 4, 2, 8, 128), BF),
             V((2, 2, 32, 8, 128), BF),
@@ -581,13 +577,13 @@
             V((64, 2, 8, 128), BF),
             pltpu.SemaphoreType.REGULAR, pltpu.SemaphoreType.REGULAR,
             dma((8,)), dma((CH,)), dma((3,)),
-            dma(()), dma((8,)),
-            dma(()), dma((3, 8)),
+            dma(()), dma((2, 8)),
+            dma(()), dma((2, 2, 8)),
             dma((4,)), dma((8,)),
             dma(()), dma(()),
             dma(()), dma(()), dma(()), dma(()),
             dma(()), dma((8,)),
-            dma(()), dma((3, 8)), dma(()), dma(()),
+            dma(()), dma((2, 8)), dma(()), dma(()),
             dma(()), dma((2, 2)), dma(()), dma(()),
             dma(()), dma((8,)), dma(()), dma(()),
         ],

time: 83.8 us -> 83.4 us (level); the launches traced: 82.6 us -> 83.2 us
  no operation moved by 1% of the time
where the time goes in v6:
time: 83.4 us; the launch traced here: 83.2 us
  Pallas kernels  80.8 us (97%)
  between operations  2.39 us (3%)
    pallas_call x1, Pallas kernels, local(): pl.pallas_call(kernel, out_shape=(S((1024, 256), BF), S((256, 2048), BF),...  76.7 us
    pallas_call x1, Pallas kernels, local(): pl.pallas_call(tail_kernel, out_shape=(S((1024, 2048), BF), S((256, 1024)...  4.08 us

profile of v6, /device:TPU:2, one launch (start us, length us, event | category | flops | bytes accessed | tf_op | source)
XLA Modules:
  0.0 83.2 jit_solution(5654267909883743729)
XLA Ops:
  0.6 76.7 %round.1 = (bf16[1024,256]{1,0:T(8,128)(2,1)}, bf16[256,2048]{1,0:T(8,128)(2,1)}, bf16[1024,256]{1,0:T(8,128)(2,1)}, f32[1]{0:T(128)}) custom-call(s32[1,256]{1,0:T(1,128)} %bitcast.3, bf16[1024,256]{1,0:T(8,128)(2,1)} %table_h.1, bf16[256,1024]{1,0:T(8,128)(2,1)} %inw_h.1, f32[1,1024]{1,0:T(1,128)} %bitcast.2, bf16[1024,2048]{1,0:T(8,128)(2,1)} %w_hbm.1, ...), custom_call_target="tpu_custom_call" | custom-call | tf_op jit(solution)/shard_map/round/pallas_call | solution.py:526
  77.3 4.1 %tail.1 = (bf16[1024,2048]{1,0:T(8,128)(2,1)}, f32[256,1024]{1,0:T(8,128)}) custom-call(bf16[1024,256]{1,0:T(8,128)(2,1)} %get-tuple-element.9.hidt, bf16[256,2048]{1,0:T(8,128)(2,1)} %get-tuple-element.10.dn, bf16[1024,256]{1,0:T(8,128)(2,1)} %get-tuple-element.11.ag), custom_call_target="tpu_custom_call" | custom-call | tf_op jit(solution)/shard_map/tail/pallas_call | solution.py:598

commit v7 on v6

--- a/solution.py
+++ b/solution.py
@@ -70,24 +70,24 @@
     return u, x, y, z, loss
 
 def tail_kernel(hidt, dn, ag, hg_o, ing_o, hv, dv, av, gv, iv, sem, osem):
-    cols = [pl.ds(i * 512, 512) for i in range(4)]
+    cols = [pl.ds(0, 256), pl.ds(256, 256)] + [pl.ds(i * 512, 512) for i in range(1, 4)]
     loads = [pltpu.make_async_copy(hidt, hv, sem.at[0])]
-    loads += [pltpu.make_async_copy(dn.at[:, cols[i]], dv.at[:, cols[i]], sem.at[1 + i]) for i in range(4)]
-    loads.append(pltpu.make_async_copy(ag, av, sem.at[5]))
+    loads += [pltpu.make_async_copy(dn.at[:, cols[i]], dv.at[:, cols[i]], sem.at[1 + i]) for i in range(5)]
+    loads.append(pltpu.make_async_copy(ag, av, sem.at[6]))
     for c in loads:
         c.start()
     loads[0].wait()
     outs = []
-    for i in range(4):
+    for i in range(5):
         loads[1 + i].wait()
         if i == 1:
-            loads[5].wait()
+            loads[6].wait()
             iv[...] = jnp.transpose(av[...].astype(F32))
         gv[:, cols[i]] = jnp.dot(hv[...], dv[:, cols[i]], preferred_element_type=F32).astype(BF)
         outs.append(pltpu.make_async_copy(gv.at[:, cols[i]], hg_o.at[:, cols[i]], osem.at[i]))
         outs[-1].start()
         if i == 1:
-            outs.append(pltpu.make_async_copy(iv, ing_o, osem.at[4]))
+            outs.append(pltpu.make_async_copy(iv, ing_o, osem.at[5]))
             outs[-1].start()
     for c in outs:
         c.wait()
@@ -320,7 +320,7 @@
         (ks[o // 2] * 2 + his[o % 2], (xz16[0][0] + los[o % 2], his[o % 2] * 2 + ks[o // 2]))
         for o in range(4)
     ]
-    for o in range(1, 4):
+    for o in (1, 3, 2):
         c_, to = members[o]
         remote(ms.at[c_], er.at[o], e1s, e1r, to).start()
     drain(na.at[pl.ds(0, 96)], gr.at[3])
@@ -353,7 +353,7 @@
     cm[32:48, :] = yy.astype(BF)
     cm[48:64, :] = jnp.zeros((16, 256), BF)
     cm[48:64, 0:16] = zz.astype(BF)
-    for o in range(1, 4):
+    for o in (1, 3, 2):
         remote(cm, cr.at[me], e2s, e2r, members[o][1]).start()
     cr[me] = cm[...]
     drain(er.at[pl.ds(1, 3)], e2r)
@@ -416,8 +416,8 @@
                     drain(like.at[pl.ds(0, 8 - n)], r4r.at[0])
 
         part, spot = g_in.at[:, zs[dz]], d_in.at[k, p, :, zs[dz]]
+        pl.when(moves)(remote(part, spot, r5s, r5r.at[1, dz], n2).start)
         pl.when(moves)(remote(part, spot, r5s, r5r.at[0, dz], n1).start)
-        pl.when(moves)(remote(part, spot, r5s, r5r.at[1, dz], n2).start)
         pl.when(stays)(remote(part, spot, r5s, r5r.at[0, dz], across).start)
 
     @pl.when(stays)
@@ -491,10 +491,18 @@
             cd[dz].wait_recv()
         rows = ag.at[pl.ds(pl.multiple_of(base + zs[(8 - dz) % 8] * 16, 16), 16)]
         for o in (4, 5, 2, 3, 6, 7, 1):
-            remote(rows, rows, p4s, p4r, peers[o][2]).start()
-    drain(a1.at[:, pl.ds(1, 7)], p4r)
+            remote(rows, rows, p4s, p4r.at[o], peers[o][2]).start()
+    def leave(x_, lo_):
+        rows = pl.ds(pl.multiple_of(x_ * 256 + lo_ * 128, 128), 128)
+        c = pltpu.make_async_copy(ag.at[rows], ag_o.at[rows], so.at[2])
+        c.start()
+
+    leave(x, lo)
+    for o in (1, 2, 6, 3, 7, 4, 5):
+        drain(a1s, p4r.at[o])
+        x_, lo_, _ = peers[8 - 2 * (o // 2) + o % 2 if o > 1 else o]
+        leave(x_, lo_)
     co.append(pltpu.make_async_copy(ag, ag_o, so.at[2]))
-    co[2].start()
 
     drain(fr, r1s)
     pl.when(stays)(pltpu.make_async_copy(r2.at[0], r2.at[0], r2s).wait)
@@ -585,7 +593,7 @@
             dma(()), dma((8,)),
             dma(()), dma((2, 8)), dma(()), dma(()),
             dma(()), dma((2, 2)), dma(()), dma(()),
-            dma(()), dma((8,)), dma(()), dma(()),
+            dma(()), dma((8,)), dma(()), dma((8,)),
         ],
         compiler_params=pltpu.CompilerParams(
             collective_id=0, has_side_effects=True, vmem_limit_bytes=60 * 1024 * 1024
@@ -603,7 +611,7 @@
         scratch_shapes=[
             V((1024, 256), BF), V((256, 2048), BF), V((1024, 256), BF),
             V((1024, 2048), BF), V((256, 1024), F32),
-            dma((6,)), dma((5,)),
+            dma((7,)), dma((6,)),
         ],
         compiler_params=pltpu.CompilerParams(vmem_limit_bytes=60 * 1024 * 1024),
         name="tail",

time: 83.4 us -> 83.5 us (level)
  no operation moved by 1% of the time
where the time goes in v7:
time: 83.5 us; the launch traced here: 83.3 us
  Pallas kernels  80.9 us (97%)
  between operations  2.39 us (3%)
    pallas_call x1, Pallas kernels, local(): pl.pallas_call(kernel, out_shape=(S((1024, 256), BF), S((256, 2048), BF),...  76.6 us
    pallas_call x1, Pallas kernels, local(): pl.pallas_call(tail_kernel, out_shape=(S((1024, 2048), BF), S((256, 1024)...  4.34 us

profile of v7, /device:TPU:2, one launch (start us, length us, event | category | flops | bytes accessed | tf_op | source)
XLA Modules:
  0.0 83.3 jit_solution(15200475726628621986)
XLA Ops:
  0.6 76.6 %round.1 = (bf16[1024,256]{1,0:T(8,128)(2,1)}, bf16[256,2048]{1,0:T(8,128)(2,1)}, bf16[1024,256]{1,0:T(8,128)(2,1)}, f32[1]{0:T(128)}) custom-call(s32[1,256]{1,0:T(1,128)} %bitcast.3, bf16[1024,256]{1,0:T(8,128)(2,1)} %table_h.1, bf16[256,1024]{1,0:T(8,128)(2,1)} %inw_h.1, f32[1,1024]{1,0:T(1,128)} %bitcast.2, bf16[1024,2048]{1,0:T(8,128)(2,1)} %w_hbm.1, ...), custom_call_target="tpu_custom_call" | custom-call | tf_op jit(solution)/shard_map/round/pallas_call | solution.py:534
  77.2 4.3 %tail.1 = (bf16[1024,2048]{1,0:T(8,128)(2,1)}, f32[256,1024]{1,0:T(8,128)}) custom-call(bf16[1024,256]{1,0:T(8,128)(2,1)} %get-tuple-element.9.hidt, bf16[256,2048]{1,0:T(8,128)(2,1)} %get-tuple-element.10.dn, bf16[1024,256]{1,0:T(8,128)(2,1)} %get-tuple-element.11.ag), custom_call_target="tpu_custom_call" | custom-call | tf_op jit(solution)/shard_map/tail/pallas_call | solution.py:606
